TPU v7x, 256 devices: a whole 4x4x8 slice. The times are simulated.
256 devices in a mesh: gx: 32 (over z, x), gy: 8 (over y, core).
Axes of the slice: x: 4, y: 4, z: 8, core: 2. Of those that a mesh axis runs over, the one named last changes fastest.
Arguments:
- fine_disp: float32 [3, 512, 128, 128], P(None, 'gx', 'gy'), may hold values from -12 to 12
- fine_prev: float32 [3, 512, 128, 128], P(None, 'gx', 'gy'), may hold values from -12 to 12
- coarse_disp: float32 [3, 256, 64, 256], P(None, 'gx', 'gy'), may hold values from -12 to 12
- coarse_prev: float32 [3, 256, 64, 256], P(None, 'gx', 'gy'), may hold values from -12 to 12
- fine_density: float32 [512, 128, 128], P('gx', 'gy'), may hold values from 0.6 to 1.8
- fine_lame: float32 [512, 128, 128], P('gx', 'gy'), may hold values from 0.5 to 2
- fine_rigidity: float32 [512, 128, 128], P('gx', 'gy'), may hold values from 0.3 to 1.5
- fine_metric: float32 [512, 128, 128], P('gx', 'gy'), may hold values from 0.7 to 1.4
- coarse_density: float32 [256, 64, 256], P('gx', 'gy'), may hold values from 0.6 to 1.8
- coarse_lame: float32 [256, 64, 256], P('gx', 'gy'), may hold values from 0.5 to 2
- coarse_rigidity: float32 [256, 64, 256], P('gx', 'gy'), may hold values from 0.3 to 1.5
- coarse_metric: float32 [256, 64, 256], P('gx', 'gy'), may hold values from 0.7 to 1.4
- offsets: int32 [2, 512, 128], P(None, 'gx', 'gy'), may hold values from -1 to 1
Outputs:
- fine_final: float32 [3, 512, 128, 128], P(None, 'gx', 'gy')
- coarse_final: float32 [3, 256, 64, 256], P(None, 'gx', 'gy')
- energy: float32 [3, 2], replicated
All inputs are finite; a program needn't handle non-finite values.
Results may differ from a plain program's by a relative error of at most 0.00021.
Values sent between devices are 32-bit elements; how exact they have to be, the bound alone decides.
A program may use at most 64 MiB of HBM per device.

v0:
```python
import jax
import jax.numpy as jnp
from jax import lax
from jax.sharding import Mesh
from jax.sharding import PartitionSpec as P

STEPS = 3
GX_GY = ("gx_0", "gx_1", "gy_0", "gy_1")
GX = ("gx_0", "gx_1")
GY = ("gy_0", "gy_1")


step_factor = 0.15


def padded(x, sides, width):
    for axis, dim in sides:
        count, length = (lax.axis_size(axis), x.shape[dim])
        up = [(i, (i + 1) % count) for i in range(count - 1)]
        down = [(j, i) for i, j in up]
        last = lax.slice_in_dim(x, length - width, length, axis=dim)
        initial = lax.slice_in_dim(x, 0, width, axis=dim)
        before = lax.ppermute(last, axis, up)
        after = lax.ppermute(initial, axis, down)
        x = jnp.concatenate([before, x, after], axis=dim)
    return x


def by_axis(x, axes):
    for axis in axes:
        x = lax.psum(x, axis)
    return x


def vertical_slope(values):
    middle = 0.5 * (values[..., 2:] - values[..., :-2])
    first = values[..., 1:2] - values[..., 0:1]
    final = values[..., -1:] - values[..., -2:-1]
    return jnp.concatenate([first, middle, final], axis=-1)


def divergence(along_x, along_y, along_z, inverse):
    return (
        0.5 * (along_x[2:] - along_x[:-2])
        + 0.5 * (along_y[:, 2:] - along_y[:, :-2])
        + inverse * vertical_slope(along_z)
    )


def interpolate(plane_ext, offsets):
    coarse_x = plane_ext.shape[1] - 4
    coarse_y = plane_ext.shape[2] - 4
    near_x = jnp.where(jnp.arange(2 * coarse_x) % 2 == 0, 0.75, 0.25)[:, None]
    near_y = jnp.where(jnp.arange(2 * coarse_y) % 2 == 0, 0.75, 0.25)[None, :]
    offset_x = offsets[0]
    offset_y = offsets[1]
    summed = jnp.zeros((3, 2 * coarse_x, 2 * coarse_y), plane_ext.dtype)
    for shift_x in (-1, 0, 1, 2):
        weight_x = jnp.where(offset_x == shift_x, near_x, 0.0) + jnp.where(
            offset_x + 1 == shift_x, 1.0 - near_x, 0.0
        )
        row_band = jnp.repeat(plane_ext[:, 2 + shift_x : 2 + shift_x + coarse_x, :], 2, axis=1)
        for shift_y in (-1, 0, 1, 2):
            weight_y = jnp.where(offset_y == shift_y, near_y, 0.0) + jnp.where(
                offset_y + 1 == shift_y, 1.0 - near_y, 0.0
            )
            tile_band = jnp.repeat(row_band[:, :, 2 + shift_y : 2 + shift_y + coarse_y], 2, axis=2)
            summed = summed + (weight_x * weight_y)[None] * tile_band
    return summed


def restrict(plane):
    half_x = plane.shape[1] // 2
    half_y = plane.shape[2] // 2
    return 0.25 * jnp.sum(plane.reshape(3, half_x, 2, half_y, 2), axis=(2, 4))


def elastic_rate(
    extended, mats_ext, div_ext, displace, top_ghost, bottom_ghost, density, lame_first, rigidity
):
    wide_ext = mats_ext[0]
    inverse = mats_ext[1, 1:-1, 1:-1]
    face_x = 0.5 * (wide_ext[:-1, 1:-1] + wide_ext[1:, 1:-1])
    flux_x = face_x * (extended[:, 1:, 1:-1] - extended[:, :-1, 1:-1])
    face_y = 0.5 * (wide_ext[1:-1, :-1] + wide_ext[1:-1, 1:])
    flux_y = face_y * (extended[:, 1:-1, 1:] - extended[:, 1:-1, :-1])
    vertical = rigidity * inverse
    face_z = jnp.concatenate(
        [vertical[:, :, :1], 0.5 * (vertical[:, :, :-1] + vertical[:, :, 1:]), vertical[:, :, -1:]],
        axis=2,
    )
    column = jnp.concatenate(
        [top_ghost[:, :, :, None], displace, bottom_ghost[:, :, :, None]], axis=3
    )
    flux_z = face_z * (column[:, :, :, 1:] - column[:, :, :, :-1])
    spread = (
        flux_x[:, 1:]
        - flux_x[:, :-1]
        + (flux_y[:, :, 1:] - flux_y[:, :, :-1])
        + (flux_z[:, :, :, 1:] - flux_z[:, :, :, :-1])
    )
    grad_x = 0.5 * (div_ext[2:, 1:-1] - div_ext[:-2, 1:-1])
    grad_y = 0.5 * (div_ext[1:-1, 2:] - div_ext[1:-1, :-2])
    grad_z = inverse * vertical_slope(div_ext[1:-1, 1:-1])
    gradient = jnp.stack([grad_x, grad_y, grad_z])
    return spread * (inverse / density) + (lame_first + rigidity) / density * gradient


def energy_part(updated, displace, rate, density, metric, cell_count):
    change = updated - displace
    inner_sum = jnp.sum(change * change - step_factor * updated * rate, axis=0)
    return jnp.sum(density * metric * inner_sum) / cell_count


def inside_mask(length, place, count):
    position = place * length + jnp.arange(length + 2) - 1
    return (position >= 0) & (position < length * count)


def wide_parts(bigger, inverse_ext, inside):
    div_full = divergence(
        bigger[0, :, 1:-1], bigger[1, 1:-1, :], bigger[2, 1:-1, 1:-1], inverse_ext
    )
    return (bigger[:, 1:-1, 1:-1], jnp.where(inside[:, :, None], div_full, 0.0))


def per_device(
    fine_disp,
    fine_prev,
    coarse_disp,
    coarse_prev,
    fine_density,
    fine_lame,
    fine_rigidity,
    fine_metric,
    coarse_density,
    coarse_lame,
    coarse_rigidity,
    coarse_metric,
    offsets,
):
    fine_mats = padded(
        jnp.stack([fine_rigidity * fine_metric, 1.0 / fine_metric]), ((GX, 1), (GY, 2)), 1
    )
    coarse_mats = padded(
        jnp.stack([coarse_rigidity * coarse_metric, 1.0 / coarse_metric]), ((GX, 1), (GY, 2)), 1
    )
    count_x = lax.axis_size(GX)
    count_y = lax.axis_size(GY)
    place_x = lax.axis_index(GX)
    place_y = lax.axis_index(GY)
    fine_cells = fine_disp.shape[1] * count_x * fine_disp.shape[2] * count_y * fine_disp.shape[3]
    coarse_cells = (
        coarse_disp.shape[1] * count_x * coarse_disp.shape[2] * count_y * coarse_disp.shape[3]
    )
    inside_fine = (
        inside_mask(fine_disp.shape[1], place_x, count_x)[:, None]
        & inside_mask(fine_disp.shape[2], place_y, count_y)[None, :]
    )
    inside_coarse = (
        inside_mask(coarse_disp.shape[1], place_x, count_x)[:, None]
        & inside_mask(coarse_disp.shape[2], place_y, count_y)[None, :]
    )
    partials = []
    for step_index in range(STEPS):
        fine_big = padded(fine_disp, ((GX, 1), (GY, 2)), 2)
        coarse_big = padded(coarse_disp, ((GX, 1), (GY, 2)), 2)
        fine_ext, fine_div_ext = wide_parts(fine_big, fine_mats[1], inside_fine)
        coarse_ext, coarse_div_ext = wide_parts(coarse_big, coarse_mats[1], inside_coarse)
        plane_ext = coarse_big[:, :, :, 0]
        fine_bottom = interpolate(plane_ext, offsets)
        fine_top = fine_disp[:, :, :, 0]
        coarse_top = restrict(fine_disp[:, :, :, -1])
        coarse_bottom = jnp.zeros_like(coarse_top)
        fine_rate = elastic_rate(
            fine_ext,
            fine_mats,
            fine_div_ext,
            fine_disp,
            fine_top,
            fine_bottom,
            fine_density,
            fine_lame,
            fine_rigidity,
        )
        coarse_rate = elastic_rate(
            coarse_ext,
            coarse_mats,
            coarse_div_ext,
            coarse_disp,
            coarse_top,
            coarse_bottom,
            coarse_density,
            coarse_lame,
            coarse_rigidity,
        )
        fine_new = 2.0 * fine_disp - fine_prev + step_factor * fine_rate
        coarse_new = 2.0 * coarse_disp - coarse_prev + step_factor * coarse_rate
        level_pair = jnp.stack(
            [
                energy_part(fine_new, fine_disp, fine_rate, fine_density, fine_metric, fine_cells),
                energy_part(
                    coarse_new,
                    coarse_disp,
                    coarse_rate,
                    coarse_density,
                    coarse_metric,
                    coarse_cells,
                ),
            ]
        )
        partials.append(level_pair)
        fine_prev, fine_disp = (fine_disp, fine_new)
        coarse_prev, coarse_disp = (coarse_disp, coarse_new)
    energy = by_axis(jnp.stack(partials), GX_GY)
    return (fine_disp, coarse_disp, energy)


def solution(mesh):
    finer = Mesh(mesh.devices.reshape(8, 4, 4, 2), ("gx_0", "gx_1", "gy_0", "gy_1"))
    in_specs = (
        P(None, GX, GY, None),
        P(None, GX, GY, None),
        P(None, GX, GY, None),
        P(None, GX, GY, None),
        P(GX, GY, None),
        P(GX, GY, None),
        P(GX, GY, None),
        P(GX, GY, None),
        P(GX, GY, None),
        P(GX, GY, None),
        P(GX, GY, None),
        P(GX, GY, None),
        P(None, GX, GY),
    )
    out_specs = (P(None, GX, GY, None), P(None, GX, GY, None), P())
    return jax.shard_map(
        per_device, mesh=finer, in_specs=in_specs, out_specs=out_specs, check_vma=False
    )
```

profile of v0, /device:TPU:1, one launch (start us, length us, event | category | flops | bytes accessed | tf_op | source)
XLA Modules:
  0.0 237.2 jit_solution(7720606352309467459)
XLA Ops:
  1.5 3.9 %collective-permute-start.5 = (f32[3,2,16,128]{3,2,1,0:T(8,128)S(1)}, f32[3,2,16,128]{3,2,1,0:T(8,128)S(1)}, u32[]{:S(2)}, u32[]{:S(2)}) collective-permute-start(f32[3,2,16,128]{3,2,1,0:T(8,128)S(1)} %get-tuple-element.84), channel_id=1, source_target_pairs={{0,8},{8,16},{16,24},{24,32},{32,40},{40,48},{48,56},{56,64},{64,7... | collective-permute-start | bytes 147464 | tf_op jit(solution)/shard_map/ppermute | solution.py:23
  6.8 1.8 fusion.134
  10.0 4.6 %collective-permute-start = (f32[2,1,16,128]{3,2,1,0:T(8,128)S(1)}, f32[2,1,16,128]{3,2,1,0:T(8,128)S(1)}, u32[]{:S(2)}, u32[]{:S(2)}) collective-permute-start(f32[2,1,16,128]{3,2,1,0:T(8,128)S(1)} %get-tuple-element.95), channel_id=1, source_target_pairs={{0,8},{8,16},{16,24},{24,32},{32,40},{40,48},{48,56},{56,64},{64,7... | collective-permute-start | bytes 49160 | tf_op jit(solution)/shard_map/ppermute | solution.py:23
  14.6 3.4 %collective-permute-start.8 = (f32[3,2,8,256]{3,2,1,0:T(8,128)S(1)}, f32[3,2,8,256]{3,2,1,0:T(8,128)S(1)}, u32[]{:S(2)}, u32[]{:S(2)}) collective-permute-start(f32[3,2,8,256]{3,2,1,0:T(8,128)S(1)} %get-tuple-element.120), channel_id=1, source_target_pairs={{0,8},{8,16},{16,24},{24,32},{32,40},{40,48},{48,56},{56,64},{64,7... | collective-permute-start | bytes 147464 | tf_op jit(solution)/shard_map/ppermute | solution.py:23
  31.3 4.0 %collective-permute-start.16 = (f32[2,1,8,256]{3,2,1,0:T(8,128)S(1)}, f32[2,1,8,256]{3,2,1,0:T(8,128)S(1)}, u32[]{:S(2)}, u32[]{:S(2)}) collective-permute-start(f32[2,1,8,256]{3,2,1,0:T(8,128)S(1)} %get-tuple-element.143), channel_id=1, source_target_pairs={{0,8},{8,16},{16,24},{24,32},{32,40},{40,48},{48,56},{56,64},{64,7... | collective-permute-start | bytes 49160 | tf_op jit(solution)/shard_map/ppermute | solution.py:23
  35.4 4.5 %collective-permute-start.3 = (f32[2,18,1,128]{3,2,1,0:T(1,128)S(1)}, f32[2,18,1,128]{3,2,1,0:T(1,128)S(1)}, u32[]{:S(2)}, u32[]{:S(2)}) collective-permute-start(f32[2,18,1,128]{3,2,1,0:T(1,128)S(1)} %get-tuple-element.92), channel_id=1, source_target_pairs={{1,0},{2,1},{3,2},{4,3},{5,4},{6,5},{7,6},{9,8},{10,9},{11,10},{12... | collective-permute-start | bytes 55304 | tf_op jit(solution)/shard_map/ppermute | solution.py:24
  39.9 3.1 %collective-permute-start.2 = (f32[2,18,1,128]{3,2,1,0:T(1,128)S(1)}, f32[2,18,1,128]{3,2,1,0:T(1,128)S(1)}, u32[]{:S(2)}, u32[]{:S(2)}) collective-permute-start(f32[2,18,1,128]{3,2,1,0:T(1,128)S(1)} %get-tuple-element.91), channel_id=1, source_target_pairs={{0,1},{1,2},{2,3},{3,4},{4,5},{5,6},{6,7},{8,9},{9,10},{10,11},{11... | collective-permute-start | bytes 55304 | tf_op jit(solution)/shard_map/ppermute | solution.py:23
  43.1 1.9 collective-permute-start.19
  45.1 3.6 %collective-permute-start.18 = (f32[2,10,1,256]{3,0,2,1:T(2,128)S(1)}, f32[2,10,1,256]{3,0,2,1:T(2,128)S(1)}, u32[]{:S(2)}, u32[]{:S(2)}) collective-permute-start(f32[2,10,1,256]{3,0,2,1:T(2,128)S(1)} %copy.352), channel_id=1, source_target_pairs={{0,1},{1,2},{2,3},{3,4},{4,5},{5,6},{6,7},{8,9},{9,10},{10,11},{11... | collective-permute-start | bytes 61448 | tf_op jit(solution)/shard_map/ppermute | solution.py:23
  50.6 1.9 collective-permute-start.6
  52.5 3.6 %collective-permute-start.7 = (f32[3,20,2,128]{3,2,1,0:T(2,128)S(1)}, f32[3,20,2,128]{3,2,1,0:T(2,128)S(1)}, u32[]{:S(2)}, u32[]{:S(2)}) collective-permute-start(f32[3,20,2,128]{3,2,1,0:T(2,128)S(1)} %get-tuple-element.71), channel_id=1, source_target_pairs={{0,1},{1,2},{2,3},{3,4},{4,5},{5,6},{6,7},{8,9},{9,10},{10,11},{11... | collective-permute-start | bytes 184328 | tf_op jit(solution)/shard_map/ppermute | solution.py:23
  56.3 1.9 collective-permute-start.11
  58.2 3.6 %collective-permute-start.10 = (f32[3,12,2,256]{3,2,1,0:T(2,128)S(1)}, f32[3,12,2,256]{3,2,1,0:T(2,128)S(1)}, u32[]{:S(2)}, u32[]{:S(2)}) collective-permute-start(f32[3,12,2,256]{3,2,1,0:T(2,128)S(1)} %get-tuple-element.89), channel_id=1, source_target_pairs={{0,1},{1,2},{2,3},{3,4},{4,5},{5,6},{6,7},{8,9},{9,10},{10,11},{11... | collective-permute-start | bytes 221192 | tf_op jit(solution)/shard_map/ppermute | solution.py:23
  79.6 5.7 %collective-permute-start.13 = (f32[3,2,16,128]{3,2,1,0:T(8,128)}, f32[3,2,16,128]{3,2,1,0:T(8,128)S(1)}, u32[]{:S(2)}, u32[]{:S(2)}) collective-permute-start(f32[3,2,16,128]{3,2,1,0:T(8,128)} %get-tuple-element.81), channel_id=1, source_target_pairs={{0,8},{8,16},{16,24},{24,32},{32,40},{40,48},{48,56},{56,64},{64,7... | collective-permute-start | bytes 147464 | tf_op jit(solution)/shard_map/ppermute | solution.py:23
  89.5 4.3 %collective-permute-start.20 = (f32[3,2,8,256]{3,2,1,0:T(8,128)S(1)}, f32[3,2,8,256]{3,2,1,0:T(8,128)S(1)}, u32[]{:S(2)}, u32[]{:S(2)}) collective-permute-start(f32[3,2,8,256]{3,2,1,0:T(8,128)S(1)} %get-tuple-element.117), channel_id=1, source_target_pairs={{0,8},{8,16},{16,24},{24,32},{32,40},{40,48},{48,56},{56,64},{64,7... | collective-permute-start | bytes 147464 | tf_op jit(solution)/shard_map/ppermute | solution.py:23
  95.1 1.9 collective-permute-start.14
  97.1 3.6 %collective-permute-start.15 = (f32[3,20,2,128]{3,2,1,0:T(2,128)S(1)}, f32[3,20,2,128]{3,2,1,0:T(2,128)S(1)}, u32[]{:S(2)}, u32[]{:S(2)}) collective-permute-start(f32[3,20,2,128]{3,2,1,0:T(2,128)S(1)} %get-tuple-element.69), channel_id=1, source_target_pairs={{0,1},{1,2},{2,3},{3,4},{4,5},{5,6},{6,7},{8,9},{9,10},{10,11},{11... | collective-permute-start | bytes 184328 | tf_op jit(solution)/shard_map/ppermute | solution.py:23
  100.8 1.9 collective-permute-start.23
  102.7 4.0 %collective-permute-start.22 = (f32[3,12,2,256]{3,2,1,0:T(2,128)S(1)}, f32[3,12,2,256]{3,2,1,0:T(2,128)S(1)}, u32[]{:S(2)}, u32[]{:S(2)}) collective-permute-start(f32[3,12,2,256]{3,2,1,0:T(2,128)S(1)} %get-tuple-element.87), channel_id=1, source_target_pairs={{0,1},{1,2},{2,3},{3,4},{4,5},{5,6},{6,7},{8,9},{9,10},{10,11},{11... | collective-permute-start | bytes 221192 | tf_op jit(solution)/shard_map/ppermute | solution.py:23
  123.0 1.6 slice_reduce_fusion
  125.9 6.2 %collective-permute-start.25 = (f32[3,2,16,128]{3,2,1,0:T(8,128)}, f32[3,2,16,128]{3,2,1,0:T(8,128)S(1)}, u32[]{:S(2)}, u32[]{:S(2)}) collective-permute-start(f32[3,2,16,128]{3,2,1,0:T(8,128)} %get-tuple-element.75), channel_id=1, source_target_pairs={{0,8},{8,16},{16,24},{24,32},{32,40},{40,48},{48,56},{56,64},{64,7... | collective-permute-start | bytes 147464 | tf_op jit(solution)/shard_map/ppermute | solution.py:23
  136.3 6.1 %collective-permute-start.28 = (f32[3,2,8,256]{3,2,1,0:T(8,128)S(1)}, f32[3,2,8,256]{3,2,1,0:T(8,128)S(1)}, u32[]{:S(2)}, u32[]{:S(2)}) collective-permute-start(f32[3,2,8,256]{3,2,1,0:T(8,128)S(1)} %get-tuple-element.115), channel_id=1, source_target_pairs={{0,8},{8,16},{16,24},{24,32},{32,40},{40,48},{48,56},{56,64},{64,7... | collective-permute-start | bytes 147464 | tf_op jit(solution)/shard_map/ppermute | solution.py:23
  145.0 1.9 collective-permute-start.26
  147.0 3.8 %collective-permute-start.27 = (f32[3,20,2,128]{3,2,1,0:T(2,128)S(1)}, f32[3,20,2,128]{3,2,1,0:T(2,128)S(1)}, u32[]{:S(2)}, u32[]{:S(2)}) collective-permute-start(f32[3,20,2,128]{3,2,1,0:T(2,128)S(1)} %get-tuple-element.68), channel_id=1, source_target_pairs={{0,1},{1,2},{2,3},{3,4},{4,5},{5,6},{6,7},{8,9},{9,10},{10,11},{11... | collective-permute-start | bytes 184328 | tf_op jit(solution)/shard_map/ppermute | solution.py:23
  150.8 1.9 collective-permute-start.31
  152.8 3.6 %collective-permute-start.30 = (f32[3,12,2,256]{3,2,1,0:T(2,128)S(1)}, f32[3,12,2,256]{3,2,1,0:T(2,128)S(1)}, u32[]{:S(2)}, u32[]{:S(2)}) collective-permute-start(f32[3,12,2,256]{3,2,1,0:T(2,128)S(1)} %get-tuple-element.85), channel_id=1, source_target_pairs={{0,1},{1,2},{2,3},{3,4},{4,5},{5,6},{6,7},{8,9},{9,10},{10,11},{11... | collective-permute-start | bytes 221192 | tf_op jit(solution)/shard_map/ppermute | solution.py:23
  171.3 1.9 subtract_reduce_fusion.5
  175.2 1.5 fusion.2
  181.7 26.6 %psum.28 = f32[3,2]{1,0:T(4,128)S(1)} all-reduce(f32[3,2]{1,0:T(4,128)S(1)} %pad_maximum_fusion.74), channel_id=1, replica_groups=mesh['gx_0'=8,'gx_1'=4,'gy_0'=4,'gy_1'=2] {'gx_0'}, use_global_device_ids=true, to_apply=%region_15.16 | all-reduce | flops 6 | bytes 48 | tf_op jit(solution)/shard_map/psum | solution.py:31
  208.3 10.8 %psum.29 = f32[3,2]{1,0:T(4,128)S(1)} all-reduce(f32[3,2]{1,0:T(4,128)S(1)} %psum.28), channel_id=1, replica_groups=mesh['gx_0'=8,'gx_1'=4,'gy_0'=4,'gy_1'=2] {'gx_1'}, use_global_device_ids=true, to_apply=%region_16.17 | all-reduce | flops 6 | bytes 48 | tf_op jit(solution)/shard_map/psum | solution.py:31
  219.0 7.3 %psum.30 = f32[3,2]{1,0:T(4,128)S(1)} all-reduce(f32[3,2]{1,0:T(4,128)S(1)} %psum.29), channel_id=1, replica_groups=mesh['gx_0'=8,'gx_1'=4,'gy_0'=4,'gy_1'=2] {'gy_0'}, use_global_device_ids=true, to_apply=%region_17.18 | all-reduce | flops 6 | bytes 48 | tf_op jit(solution)/shard_map/psum | solution.py:31
  226.3 10.3 %psum.31 = f32[3,2]{1,0:T(4,128)S(1)} all-reduce(f32[3,2]{1,0:T(4,128)S(1)} %psum.30), channel_id=1, replica_groups=mesh['gx_0'=8,'gx_1'=4,'gy_0'=4,'gy_1'=2] {'gy_1'}, use_global_device_ids=true, to_apply=%region_18.19 | all-reduce | flops 6 | bytes 48 | tf_op jit(solution)/shard_map/psum | solution.py:31
  (664 shorter events, 82.8 us)
Async XLA Ops:
  1.5 49.0 %collective-permute-start.5 = (f32[3,2,16,128]{3,2,1,0:T(8,128)S(1)}, f32[3,2,16,128]{3,2,1,0:T(8,128)S(1)}, u32[]{:S(2)}, u32[]{:S(2)}) collective-permute-start(f32[3,2,16,128]{3,2,1,0:T(8,128)S(1)} %get-tuple-element.84), channel_id=1, source_target_pairs={{0,8},{8,16},{16,24},{24,32},{32,40},{40,48},{48,56},{56,64},{64,7... | collective-permute-start | bytes 147464 | tf_op jit(solution)/shard_map/ppermute | solution.py:23
  5.4 45.1 %collective-permute-start.4 = (f32[3,2,16,128]{3,2,1,0:T(8,128)S(1)}, f32[3,2,16,128]{3,2,1,0:T(8,128)S(1)}, u32[]{:S(2)}, u32[]{:S(2)}) collective-permute-start(f32[3,2,16,128]{3,2,1,0:T(8,128)S(1)} %get-tuple-element.83), channel_id=1, source_target_pairs={{8,0},{16,8},{24,16},{32,24},{40,32},{48,40},{56,48},{64,56},{72,6... | collective-permute-start | bytes 147464 | tf_op jit(solution)/shard_map/ppermute | solution.py:24
  8.5 21.5 %collective-permute-start.1 = (f32[2,1,16,128]{3,2,1,0:T(8,128)S(1)}, f32[2,1,16,128]{3,2,1,0:T(8,128)S(1)}, u32[]{:S(2)}, u32[]{:S(2)}) collective-permute-start(f32[2,1,16,128]{3,2,1,0:T(8,128)S(1)} %get-tuple-element.96), channel_id=1, source_target_pairs={{8,0},{16,8},{24,16},{32,24},{40,32},{48,40},{56,48},{64,56},{72,6... | collective-permute-start | bytes 49160 | tf_op jit(solution)/shard_map/ppermute | solution.py:24
  10.0 21.3 %collective-permute-start = (f32[2,1,16,128]{3,2,1,0:T(8,128)S(1)}, f32[2,1,16,128]{3,2,1,0:T(8,128)S(1)}, u32[]{:S(2)}, u32[]{:S(2)}) collective-permute-start(f32[2,1,16,128]{3,2,1,0:T(8,128)S(1)} %get-tuple-element.95), channel_id=1, source_target_pairs={{0,8},{8,16},{16,24},{24,32},{32,40},{40,48},{48,56},{56,64},{64,7... | collective-permute-start | bytes 49160 | tf_op jit(solution)/shard_map/ppermute | solution.py:23
  14.6 41.6 %collective-permute-start.8 = (f32[3,2,8,256]{3,2,1,0:T(8,128)S(1)}, f32[3,2,8,256]{3,2,1,0:T(8,128)S(1)}, u32[]{:S(2)}, u32[]{:S(2)}) collective-permute-start(f32[3,2,8,256]{3,2,1,0:T(8,128)S(1)} %get-tuple-element.120), channel_id=1, source_target_pairs={{0,8},{8,16},{16,24},{24,32},{32,40},{40,48},{48,56},{56,64},{64,7... | collective-permute-start | bytes 147464 | tf_op jit(solution)/shard_map/ppermute | solution.py:23
  30.0 5.3 %collective-permute-start.17 = (f32[2,1,8,256]{3,2,1,0:T(8,128)S(1)}, f32[2,1,8,256]{3,2,1,0:T(8,128)S(1)}, u32[]{:S(2)}, u32[]{:S(2)}) collective-permute-start(f32[2,1,8,256]{3,2,1,0:T(8,128)S(1)} %get-tuple-element.144), channel_id=1, source_target_pairs={{8,0},{16,8},{24,16},{32,24},{40,32},{48,40},{56,48},{64,56},{72,6... | collective-permute-start | bytes 49160 | tf_op jit(solution)/shard_map/ppermute | solution.py:24
  31.3 8.6 %collective-permute-start.16 = (f32[2,1,8,256]{3,2,1,0:T(8,128)S(1)}, f32[2,1,8,256]{3,2,1,0:T(8,128)S(1)}, u32[]{:S(2)}, u32[]{:S(2)}) collective-permute-start(f32[2,1,8,256]{3,2,1,0:T(8,128)S(1)} %get-tuple-element.143), channel_id=1, source_target_pairs={{0,8},{8,16},{16,24},{24,32},{32,40},{40,48},{48,56},{56,64},{64,7... | collective-permute-start | bytes 49160 | tf_op jit(solution)/shard_map/ppermute | solution.py:23
  35.4 7.8 %collective-permute-start.3 = (f32[2,18,1,128]{3,2,1,0:T(1,128)S(1)}, f32[2,18,1,128]{3,2,1,0:T(1,128)S(1)}, u32[]{:S(2)}, u32[]{:S(2)}) collective-permute-start(f32[2,18,1,128]{3,2,1,0:T(1,128)S(1)} %get-tuple-element.92), channel_id=1, source_target_pairs={{1,0},{2,1},{3,2},{4,3},{5,4},{6,5},{7,6},{9,8},{10,9},{11,10},{12... | collective-permute-start | bytes 55304 | tf_op jit(solution)/shard_map/ppermute | solution.py:24
  39.9 5.1 %collective-permute-start.2 = (f32[2,18,1,128]{3,2,1,0:T(1,128)S(1)}, f32[2,18,1,128]{3,2,1,0:T(1,128)S(1)}, u32[]{:S(2)}, u32[]{:S(2)}) collective-permute-start(f32[2,18,1,128]{3,2,1,0:T(1,128)S(1)} %get-tuple-element.91), channel_id=1, source_target_pairs={{0,1},{1,2},{2,3},{3,4},{4,5},{5,6},{6,7},{8,9},{9,10},{10,11},{11... | collective-permute-start | bytes 55304 | tf_op jit(solution)/shard_map/ppermute | solution.py:23
  43.1 5.8 %collective-permute-start.19 = (f32[2,10,1,256]{3,0,2,1:T(2,128)S(1)}, f32[2,10,1,256]{3,0,2,1:T(2,128)S(1)}, u32[]{:S(2)}, u32[]{:S(2)}) collective-permute-start(f32[2,10,1,256]{3,0,2,1:T(2,128)S(1)} %copy.353), channel_id=1, source_target_pairs={{1,0},{2,1},{3,2},{4,3},{5,4},{6,5},{7,6},{9,8},{10,9},{11,10},{12... | collective-permute-start | bytes 61448 | tf_op jit(solution)/shard_map/ppermute | solution.py:24
  45.1 5.2 %collective-permute-start.18 = (f32[2,10,1,256]{3,0,2,1:T(2,128)S(1)}, f32[2,10,1,256]{3,0,2,1:T(2,128)S(1)}, u32[]{:S(2)}, u32[]{:S(2)}) collective-permute-start(f32[2,10,1,256]{3,0,2,1:T(2,128)S(1)} %copy.352), channel_id=1, source_target_pairs={{0,1},{1,2},{2,3},{3,4},{4,5},{5,6},{6,7},{8,9},{9,10},{10,11},{11... | collective-permute-start | bytes 61448 | tf_op jit(solution)/shard_map/ppermute | solution.py:23
  48.9 7.3 %collective-permute-start.9 = (f32[3,2,8,256]{3,2,1,0:T(8,128)S(1)}, f32[3,2,8,256]{3,2,1,0:T(8,128)S(1)}, u32[]{:S(2)}, u32[]{:S(2)}) collective-permute-start(f32[3,2,8,256]{3,2,1,0:T(8,128)S(1)} %get-tuple-element.119), channel_id=1, source_target_pairs={{8,0},{16,8},{24,16},{32,24},{40,32},{48,40},{56,48},{64,56},{72,6... | collective-permute-start | bytes 147464 | tf_op jit(solution)/shard_map/ppermute | solution.py:24
  50.6 12.1 %collective-permute-start.6 = (f32[3,20,2,128]{3,2,1,0:T(2,128)S(1)}, f32[3,20,2,128]{3,2,1,0:T(2,128)S(1)}, u32[]{:S(2)}, u32[]{:S(2)}) collective-permute-start(f32[3,20,2,128]{3,2,1,0:T(2,128)S(1)} %get-tuple-element.72), channel_id=1, source_target_pairs={{1,0},{2,1},{3,2},{4,3},{5,4},{6,5},{7,6},{9,8},{10,9},{11,10},{12... | collective-permute-start | bytes 184328 | tf_op jit(solution)/shard_map/ppermute | solution.py:24
  52.5 10.2 %collective-permute-start.7 = (f32[3,20,2,128]{3,2,1,0:T(2,128)S(1)}, f32[3,20,2,128]{3,2,1,0:T(2,128)S(1)}, u32[]{:S(2)}, u32[]{:S(2)}) collective-permute-start(f32[3,20,2,128]{3,2,1,0:T(2,128)S(1)} %get-tuple-element.71), channel_id=1, source_target_pairs={{0,1},{1,2},{2,3},{3,4},{4,5},{5,6},{6,7},{8,9},{9,10},{10,11},{11... | collective-permute-start | bytes 184328 | tf_op jit(solution)/shard_map/ppermute | solution.py:23
  56.3 10.0 %collective-permute-start.11 = (f32[3,12,2,256]{3,2,1,0:T(2,128)S(1)}, f32[3,12,2,256]{3,2,1,0:T(2,128)S(1)}, u32[]{:S(2)}, u32[]{:S(2)}) collective-permute-start(f32[3,12,2,256]{3,2,1,0:T(2,128)S(1)} %get-tuple-element.90), channel_id=1, source_target_pairs={{1,0},{2,1},{3,2},{4,3},{5,4},{6,5},{7,6},{9,8},{10,9},{11,10},{12... | collective-permute-start | bytes 221192 | tf_op jit(solution)/shard_map/ppermute | solution.py:24
  58.2 8.1 %collective-permute-start.10 = (f32[3,12,2,256]{3,2,1,0:T(2,128)S(1)}, f32[3,12,2,256]{3,2,1,0:T(2,128)S(1)}, u32[]{:S(2)}, u32[]{:S(2)}) collective-permute-start(f32[3,12,2,256]{3,2,1,0:T(2,128)S(1)} %get-tuple-element.89), channel_id=1, source_target_pairs={{0,1},{1,2},{2,3},{3,4},{4,5},{5,6},{6,7},{8,9},{9,10},{10,11},{11... | collective-permute-start | bytes 221192 | tf_op jit(solution)/shard_map/ppermute | solution.py:23
  78.3 16.7 %collective-permute-start.12 = (f32[3,2,16,128]{3,2,1,0:T(8,128)}, f32[3,2,16,128]{3,2,1,0:T(8,128)S(1)}, u32[]{:S(2)}, u32[]{:S(2)}) collective-permute-start(f32[3,2,16,128]{3,2,1,0:T(8,128)} %get-tuple-element.82), channel_id=1, source_target_pairs={{8,0},{16,8},{24,16},{32,24},{40,32},{48,40},{56,48},{64,56},{72,6... | collective-permute-start | bytes 147464 | tf_op jit(solution)/shard_map/ppermute | solution.py:24
  79.6 15.4 %collective-permute-start.13 = (f32[3,2,16,128]{3,2,1,0:T(8,128)}, f32[3,2,16,128]{3,2,1,0:T(8,128)S(1)}, u32[]{:S(2)}, u32[]{:S(2)}) collective-permute-start(f32[3,2,16,128]{3,2,1,0:T(8,128)} %get-tuple-element.81), channel_id=1, source_target_pairs={{0,8},{8,16},{16,24},{24,32},{32,40},{40,48},{48,56},{56,64},{64,7... | collective-permute-start | bytes 147464 | tf_op jit(solution)/shard_map/ppermute | solution.py:23
  88.2 12.5 %collective-permute-start.21 = (f32[3,2,8,256]{3,2,1,0:T(8,128)S(1)}, f32[3,2,8,256]{3,2,1,0:T(8,128)S(1)}, u32[]{:S(2)}, u32[]{:S(2)}) collective-permute-start(f32[3,2,8,256]{3,2,1,0:T(8,128)S(1)} %get-tuple-element.118), channel_id=1, source_target_pairs={{8,0},{16,8},{24,16},{32,24},{40,32},{48,40},{56,48},{64,56},{72,6... | collective-permute-start | bytes 147464 | tf_op jit(solution)/shard_map/ppermute | solution.py:24
  89.5 11.2 %collective-permute-start.20 = (f32[3,2,8,256]{3,2,1,0:T(8,128)S(1)}, f32[3,2,8,256]{3,2,1,0:T(8,128)S(1)}, u32[]{:S(2)}, u32[]{:S(2)}) collective-permute-start(f32[3,2,8,256]{3,2,1,0:T(8,128)S(1)} %get-tuple-element.117), channel_id=1, source_target_pairs={{0,8},{8,16},{16,24},{24,32},{32,40},{40,48},{48,56},{56,64},{64,7... | collective-permute-start | bytes 147464 | tf_op jit(solution)/shard_map/ppermute | solution.py:23
  95.1 12.4 %collective-permute-start.14 = (f32[3,20,2,128]{3,2,1,0:T(2,128)S(1)}, f32[3,20,2,128]{3,2,1,0:T(2,128)S(1)}, u32[]{:S(2)}, u32[]{:S(2)}) collective-permute-start(f32[3,20,2,128]{3,2,1,0:T(2,128)S(1)} %get-tuple-element.70), channel_id=1, source_target_pairs={{1,0},{2,1},{3,2},{4,3},{5,4},{6,5},{7,6},{9,8},{10,9},{11,10},{12... | collective-permute-start | bytes 184328 | tf_op jit(solution)/shard_map/ppermute | solution.py:24
  97.1 10.5 %collective-permute-start.15 = (f32[3,20,2,128]{3,2,1,0:T(2,128)S(1)}, f32[3,20,2,128]{3,2,1,0:T(2,128)S(1)}, u32[]{:S(2)}, u32[]{:S(2)}) collective-permute-start(f32[3,20,2,128]{3,2,1,0:T(2,128)S(1)} %get-tuple-element.69), channel_id=1, source_target_pairs={{0,1},{1,2},{2,3},{3,4},{4,5},{5,6},{6,7},{8,9},{9,10},{10,11},{11... | collective-permute-start | bytes 184328 | tf_op jit(solution)/shard_map/ppermute | solution.py:23
  100.8 11.2 %collective-permute-start.23 = (f32[3,12,2,256]{3,2,1,0:T(2,128)S(1)}, f32[3,12,2,256]{3,2,1,0:T(2,128)S(1)}, u32[]{:S(2)}, u32[]{:S(2)}) collective-permute-start(f32[3,12,2,256]{3,2,1,0:T(2,128)S(1)} %get-tuple-element.88), channel_id=1, source_target_pairs={{1,0},{2,1},{3,2},{4,3},{5,4},{6,5},{7,6},{9,8},{10,9},{11,10},{12... | collective-permute-start | bytes 221192 | tf_op jit(solution)/shard_map/ppermute | solution.py:24
  102.7 9.3 %collective-permute-start.22 = (f32[3,12,2,256]{3,2,1,0:T(2,128)S(1)}, f32[3,12,2,256]{3,2,1,0:T(2,128)S(1)}, u32[]{:S(2)}, u32[]{:S(2)}) collective-permute-start(f32[3,12,2,256]{3,2,1,0:T(2,128)S(1)} %get-tuple-element.87), channel_id=1, source_target_pairs={{0,1},{1,2},{2,3},{3,4},{4,5},{5,6},{6,7},{8,9},{9,10},{10,11},{11... | collective-permute-start | bytes 221192 | tf_op jit(solution)/shard_map/ppermute | solution.py:23
  124.6 19.8 %collective-permute-start.24 = (f32[3,2,16,128]{3,2,1,0:T(8,128)}, f32[3,2,16,128]{3,2,1,0:T(8,128)S(1)}, u32[]{:S(2)}, u32[]{:S(2)}) collective-permute-start(f32[3,2,16,128]{3,2,1,0:T(8,128)} %get-tuple-element.76), channel_id=1, source_target_pairs={{8,0},{16,8},{24,16},{32,24},{40,32},{48,40},{56,48},{64,56},{72,6... | collective-permute-start | bytes 147464 | tf_op jit(solution)/shard_map/ppermute | solution.py:24
  125.9 18.5 %collective-permute-start.25 = (f32[3,2,16,128]{3,2,1,0:T(8,128)}, f32[3,2,16,128]{3,2,1,0:T(8,128)S(1)}, u32[]{:S(2)}, u32[]{:S(2)}) collective-permute-start(f32[3,2,16,128]{3,2,1,0:T(8,128)} %get-tuple-element.75), channel_id=1, source_target_pairs={{0,8},{8,16},{16,24},{24,32},{32,40},{40,48},{48,56},{56,64},{64,7... | collective-permute-start | bytes 147464 | tf_op jit(solution)/shard_map/ppermute | solution.py:23
  135.0 15.8 %collective-permute-start.29 = (f32[3,2,8,256]{3,2,1,0:T(8,128)S(1)}, f32[3,2,8,256]{3,2,1,0:T(8,128)S(1)}, u32[]{:S(2)}, u32[]{:S(2)}) collective-permute-start(f32[3,2,8,256]{3,2,1,0:T(8,128)S(1)} %get-tuple-element.116), channel_id=1, source_target_pairs={{8,0},{16,8},{24,16},{32,24},{40,32},{48,40},{56,48},{64,56},{72,6... | collective-permute-start | bytes 147464 | tf_op jit(solution)/shard_map/ppermute | solution.py:24
  136.3 14.5 %collective-permute-start.28 = (f32[3,2,8,256]{3,2,1,0:T(8,128)S(1)}, f32[3,2,8,256]{3,2,1,0:T(8,128)S(1)}, u32[]{:S(2)}, u32[]{:S(2)}) collective-permute-start(f32[3,2,8,256]{3,2,1,0:T(8,128)S(1)} %get-tuple-element.115), channel_id=1, source_target_pairs={{0,8},{8,16},{16,24},{24,32},{32,40},{40,48},{48,56},{56,64},{64,7... | collective-permute-start | bytes 147464 | tf_op jit(solution)/shard_map/ppermute | solution.py:23
  145.0 12.2 %collective-permute-start.26 = (f32[3,20,2,128]{3,2,1,0:T(2,128)S(1)}, f32[3,20,2,128]{3,2,1,0:T(2,128)S(1)}, u32[]{:S(2)}, u32[]{:S(2)}) collective-permute-start(f32[3,20,2,128]{3,2,1,0:T(2,128)S(1)} %get-tuple-element.67), channel_id=1, source_target_pairs={{1,0},{2,1},{3,2},{4,3},{5,4},{6,5},{7,6},{9,8},{10,9},{11,10},{12... | collective-permute-start | bytes 184328 | tf_op jit(solution)/shard_map/ppermute | solution.py:24
  147.0 10.3 %collective-permute-start.27 = (f32[3,20,2,128]{3,2,1,0:T(2,128)S(1)}, f32[3,20,2,128]{3,2,1,0:T(2,128)S(1)}, u32[]{:S(2)}, u32[]{:S(2)}) collective-permute-start(f32[3,20,2,128]{3,2,1,0:T(2,128)S(1)} %get-tuple-element.68), channel_id=1, source_target_pairs={{0,1},{1,2},{2,3},{3,4},{4,5},{5,6},{6,7},{8,9},{9,10},{10,11},{11... | collective-permute-start | bytes 184328 | tf_op jit(solution)/shard_map/ppermute | solution.py:23
  150.8 11.0 %collective-permute-start.31 = (f32[3,12,2,256]{3,2,1,0:T(2,128)S(1)}, f32[3,12,2,256]{3,2,1,0:T(2,128)S(1)}, u32[]{:S(2)}, u32[]{:S(2)}) collective-permute-start(f32[3,12,2,256]{3,2,1,0:T(2,128)S(1)} %get-tuple-element.86), channel_id=1, source_target_pairs={{1,0},{2,1},{3,2},{4,3},{5,4},{6,5},{7,6},{9,8},{10,9},{11,10},{12... | collective-permute-start | bytes 221192 | tf_op jit(solution)/shard_map/ppermute | solution.py:24
  152.8 9.0 %collective-permute-start.30 = (f32[3,12,2,256]{3,2,1,0:T(2,128)S(1)}, f32[3,12,2,256]{3,2,1,0:T(2,128)S(1)}, u32[]{:S(2)}, u32[]{:S(2)}) collective-permute-start(f32[3,12,2,256]{3,2,1,0:T(2,128)S(1)} %get-tuple-element.85), channel_id=1, source_target_pairs={{0,1},{1,2},{2,3},{3,4},{4,5},{5,6},{6,7},{8,9},{9,10},{10,11},{11... | collective-permute-start | bytes 221192 | tf_op jit(solution)/shard_map/ppermute | solution.py:23
  (162 other events, 1081.8 us)
where the time goes:
time: 239 us; the launch traced here: 237 us
  starting transfers between devices  95.6 us (40%)
  blocking collectives  54.9 us (23%)
  other arithmetic  39.9 us (17%)
  local copies, waits for them, and re-layouts  39.2 us (16%)
  between operations  7.58 us (3%)
    ppermute x16, starting transfers between devices, padded(): before = lax.ppermute(last, axis, up)  67.2 us
    psum x4, blocking collectives, by_axis(): x = lax.psum(x, axis)  54.9 us
    ppermute x16, starting transfers between devices, padded(): after = lax.ppermute(initial, axis, down)  28.4 us
    unnamed x328, local copies, waits for them, and re-layouts  18.2 us
    another operation x12, other arithmetic, elastic_rate(): gradient = jnp.stack([grad_x, grad_y, grad_z])  6.96 us
    mul x16, local copies, waits for them, and re-layouts, interpolate(): summed = summed + (weight_x * weight_y)[None] * tile_band  6.48 us
    mul x6, other arithmetic, elastic_rate(): flux_z = face_z * (column[:, :, :, 1:] - column[:, :, :, :-1])  5.73 us
  transfers between devices with their start and end apart: 32, of which 0 were waited for; matrix products, arithmetic and copies ran while one was open for 13% of the time, Pallas kernels for 0%

commit v1 on v0

v1 whole, which is shorter than its diff:
```python
import functools

import jax
import jax.numpy as jnp
from jax import lax
from jax.experimental import pallas as pl
from jax.experimental.pallas import tpu as pltpu
from jax.sharding import PartitionSpec as P

STEPS = 3
DT = 0.15
MESH = pl.DeviceIdType.MESH
F32 = jnp.float32

R = 2
LO, HI = 0, 1
(WIDE, HALF_A, ISV, GB, GZ, DM, CZU, CZD, CXP, CXM, CYU, CYD, C0) = range(13)
NCOEF = 13


def lanes(shape):
    return lax.broadcasted_iota(jnp.int32, shape, len(shape) - 1)


def subs(shape):
    return lax.broadcasted_iota(jnp.int32, shape, len(shape) - 2)


def spread_row(row):
    return jnp.broadcast_to(row, (8, 128))


def roll(x, shift, axis):
    return pltpu.roll(x, shift % x.shape[axis], axis)


class Fine:
    n = 16
    key = "f"

    @staticmethod
    def load(ref, i, r):
        parts = [ref[pl.ds(16 * i + t, 8 * r, stride=2), :].reshape(1, r, 8, 128) for t in (0, 1)]
        return jnp.concatenate(parts, axis=0)

    @staticmethod
    def store(ref, i, r, value):
        for t in (0, 1):
            ref[pl.ds(16 * i + t, 8 * r, stride=2), :] = value[t].reshape(8 * r, 128)

    @staticmethod
    def k_up(x, last=None):
        moved = roll(x, -1, 3)
        edge = x if last is None else last
        return jnp.where(lanes(x.shape) == 127, edge, moved)

    @staticmethod
    def k_down(x, first=None):
        moved = roll(x, 1, 3)
        edge = x if first is None else first
        return jnp.where(lanes(x.shape) == 0, edge, moved)

    @staticmethod
    def edge_scale(shape):
        k = lanes(shape)
        return jnp.where((k == 0) | (k == 127), 1.0, 0.5).astype(F32)

    @staticmethod
    def row_of(ref, i, r):
        return jnp.concatenate(
            [spread_row(ref[pl.ds(i + m, 1), :]).reshape(1, 8, 128) for m in range(r)], axis=0
        )

    @staticmethod
    def j_up(x, halo):
        s = subs(x.shape[1:])
        moved = jnp.where(s == 7, halo, roll(x[0], -1, 1))
        return jnp.stack([x[1], moved])

    @staticmethod
    def j_down(x, halo):
        s = subs(x.shape[1:])
        moved = jnp.where(s == 0, halo, roll(x[1], 1, 1))
        return jnp.stack([moved, x[0]])

    @staticmethod
    def plane(ref, j):
        return jnp.concatenate([ref[pl.ds(j + 128 * h, 8, stride=16), :] for h in (0, 1)], axis=0)

    @staticmethod
    def plane_k_up(x):
        return jnp.where(lanes(x.shape) == 127, x, roll(x, -1, 1))

    @staticmethod
    def plane_k_down(x):
        return jnp.where(lanes(x.shape) == 0, x, roll(x, 1, 1))

    @staticmethod
    def corner(tile_ref, comp):
        return spread_row(tile_ref[pl.ds(comp, 1), :])

    @staticmethod
    def corner_plane(tile_ref, comp):
        row = spread_row(tile_ref[pl.ds(comp, 1), :])
        return jnp.concatenate([row, row], axis=0)

    @staticmethod
    def corner_row(tile_ref, comp):
        return spread_row(tile_ref[pl.ds(comp, 1), :]).reshape(1, 8, 128)


class Coarse:
    n = 8
    key = "c"

    @staticmethod
    def load(ref, i, r):
        return ref[:, pl.ds(8 * i, 8 * r), :].reshape(2, r, 8, 128)

    @staticmethod
    def store(ref, i, r, value):
        ref[:, pl.ds(8 * i, 8 * r), :] = value.reshape(2, 8 * r, 128)

    @staticmethod
    def k_up(x, last=None):
        moved = roll(x, -1, 3)
        edge = x[1] if last is None else last
        return jnp.where(lanes(x.shape) == 127, jnp.stack([moved[1], edge]), moved)

    @staticmethod
    def k_down(x, first=None):
        moved = roll(x, 1, 3)
        edge = x[0] if first is None else first
        return jnp.where(lanes(x.shape) == 0, jnp.stack([edge, moved[0]]), moved)

    @staticmethod
    def edge_scale(shape):
        k = lanes(shape)
        half = lax.broadcasted_iota(jnp.int32, shape, 0)
        ends = ((k == 0) & (half == 0)) | ((k == 127) & (half == 1))
        return jnp.where(ends, 1.0, 0.5).astype(F32)

    @staticmethod
    def row_of(ref, i, r):
        halves = []
        for h in (0, 1):
            rows = [spread_row(ref[h, pl.ds(i + m, 1), :]).reshape(1, 8, 128) for m in range(r)]
            halves.append(jnp.concatenate(rows, axis=0))
        return jnp.stack(halves)

    @staticmethod
    def j_up(x, halo):
        return jnp.where(subs(x.shape) == 7, halo, roll(x, -1, 2))

    @staticmethod
    def j_down(x, halo):
        return jnp.where(subs(x.shape) == 0, halo, roll(x, 1, 2))

    @staticmethod
    def plane(ref, j):
        return jnp.stack([ref[h, pl.ds(j, 8, stride=8), :] for h in (0, 1)])

    @staticmethod
    def plane_k_up(x):
        return Coarse.k_up(x[:, None])[:, 0]

    @staticmethod
    def plane_k_down(x):
        return Coarse.k_down(x[:, None])[:, 0]

    @staticmethod
    def corner_plane(tile_ref, comp):
        return jnp.stack([spread_row(tile_ref[pl.ds(2 + 2 * comp + h, 1), :]) for h in (0, 1)])

    @staticmethod
    def corner_row(tile_ref, comp):
        rows = [spread_row(tile_ref[pl.ds(2 + 2 * comp + h, 1), :]) for h in (0, 1)]
        return jnp.stack(rows)[:, None]


def plane_roll(level, x, shift):
    return roll(x, shift, 0) if level is Fine else roll(x, shift, 1)


def plane_sub(level, x):
    return subs(x.shape)


def neighbour_rows(level, ref, i, r, step, halo):
    if step > 0:
        if i + r < level.n:
            return level.load(ref, i + 1, r)
        return jnp.concatenate([level.load(ref, i + 1, r - 1), halo()], axis=1)
    if i > 0:
        return level.load(ref, i - 1, r)
    return jnp.concatenate([halo(), level.load(ref, 0, r - 1)], axis=1)


def kernel(nx, ny, group_x, *refs):
    names_in = (
        "fine_disp fine_prev coarse_disp coarse_prev fine_density fine_lame fine_rigidity"
        " fine_metric coarse_density coarse_lame coarse_rigidity coarse_metric"
    ).split()
    hbm = dict(zip(names_in, refs[:12]))
    offsets_ref = refs[12]
    fine_out, coarse_out, energy_out = refs[13:16]
    (
        uf, uc, matf, matc, kf, kc, dvf, dvc, dyf, dyc,
        xhf, xhc, yhf, yhc, ysf, ysc, xmf, xmc, ymf, ymc, ysmf, ysmc,
        pls, plx, ply, cos, cor, weights, ghost, eacc, erow, er1, er2,
        load_sem, out_sem, send_sem, recv_sem, esend, erecv,
    ) = refs[16:]

    gx, gy = lax.axis_index("gx"), lax.axis_index("gy")
    exists = {
        (dx, dy): functools.reduce(
            jnp.logical_and,
            ([gx > 0] if dx < 0 else [gx < nx - 1] if dx > 0 else [])
            + ([gy > 0] if dy < 0 else [gy < ny - 1] if dy > 0 else []),
        )
        for dx in (-1, 0, 1)
        for dy in (-1, 0, 1)
        if (dx, dy) != (0, 0)
    }
    directions = list(exists)
    corners = [d for d in directions if d[0] and d[1]]
    corner_id = {d: n for n, d in enumerate(corners)}

    def flag(direction):
        return jnp.where(exists[direction], 1.0, 0.0).astype(F32)

    def device(direction):
        return {"gx": gx + direction[0], "gy": gy + direction[1]}

    groups = nx // group_x
    gx_hi, gx_lo = gx // group_x, gx % group_x
    n1, n2 = group_x * ny, groups
    me1 = gx_lo * ny + gy

    def peer1(d):
        q = lax.rem(me1 + d, n1)
        return {"gx": gx_hi * group_x + q // ny, "gy": q % ny}

    def peer2(d):
        return {"gx": lax.rem(gx_hi + d, n2) * group_x + gx_lo, "gy": gy}

    barrier = pltpu.get_barrier_semaphore()
    for d in directions:
        @pl.when(exists[d])
        def _(d=d):
            pl.semaphore_signal(barrier, inc=1, device_id=device(d), device_id_type=MESH)

    @pl.loop(1, n1)
    def _(d):
        pl.semaphore_signal(barrier, inc=1, device_id=peer1(d), device_id_type=MESH)

    if n2 > 1:
        @pl.loop(1, n2)
        def _(d):
            pl.semaphore_signal(barrier, inc=1, device_id=peer2(d), device_id_type=MESH)

    loads = {}

    def start_load(name, dst, sem):
        fine = name.startswith("fine")
        src = hbm[name]
        if fine:
            copies = [pltpu.make_async_copy(src, dst, load_sem.at[sem, 0])]
        else:
            lead = (slice(None),) * (len(src.shape) - 2)
            copies = [
                pltpu.make_async_copy(
                    src.at[lead + (slice(None), pl.ds(128 * h, 128))],
                    dst.at[(slice(None), h) if lead else (h,)],
                    load_sem.at[sem, h],
                )
                for h in (0, 1)
            ]
        for c in copies:
            c.start()
        loads[name] = copies

    plan = [
        ("fine_disp", uf.at[1]), ("coarse_disp", uc.at[1]),
        ("fine_rigidity", matf.at[0]), ("coarse_rigidity", matc.at[0]),
        ("fine_metric", matf.at[1]), ("coarse_metric", matc.at[1]),
        ("fine_density", matf.at[2]), ("fine_lame", matf.at[3]),
        ("coarse_density", matc.at[2]), ("coarse_lame", matc.at[3]),
        ("fine_prev", uf.at[0]), ("coarse_prev", uc.at[0]),
    ]
    for sem, (name, dst) in enumerate(plan):
        start_load(name, dst, sem)

    def wait_load(*names):
        for name in names:
            for c in loads[name]:
                c.wait()

    side_of = {-1: LO, 1: HI}

    def messages(s):
        out = []
        u_f, u_c = uf.at[s + 1], uc.at[s + 1]
        for dx in (-1, 1):
            own, far = side_of[dx], side_of[-dx]
            first, second = (0, 1) if dx < 0 else (15, 14)
            out.append(("fx", (dx, 0), u_f.at[:, pl.ds(16 * first, 16)], xhf.at[s, far, pl.ds(0, 3)]))
            out.append(("fx", (dx, 0), u_f.at[0, pl.ds(16 * second, 16)], xhf.at[s, far, 3]))
            first, second = (0, 1) if dx < 0 else (7, 6)
            out.append(("cx", (dx, 0), u_c.at[:, :, pl.ds(8 * first, 8)], xhc.at[s, far, pl.ds(0, 3)]))
            out.append(("cx", (dx, 0), u_c.at[0, :, pl.ds(8 * second, 8)], xhc.at[s, far, 3]))
            out.append(("cp", (dx, 0), pls.at[s], plx.at[s, far]))
            if s == 0:
                first = 0 if dx < 0 else 15
                out.append(("mx", (dx, 0), matf.at[pl.ds(0, 2), pl.ds(16 * first, 16)], xmf.at[far]))
                first = 0 if dx < 0 else 7
                out.append(("mx", (dx, 0), matc.at[pl.ds(0, 2), :, pl.ds(8 * first, 8)], xmc.at[far]))
        for dy in (-1, 1):
            own, far = side_of[dy], side_of[-dy]
            out.append(("fy", (0, dy), ysf.at[s, own], yhf.at[s, far]))
            out.append(("cy", (0, dy), ysc.at[s, own], yhc.at[s, far]))
            out.append(("cp", (0, dy), pls.at[s], ply.at[s, far]))
            if s == 0:
                out.append(("my", (0, dy), ysmf.at[own], ymf.at[far]))
                out.append(("my", (0, dy), ysmc.at[own], ymc.at[far]))
        for d in corners:
            back = corner_id[(-d[0], -d[1])]
            out.append(("co", d, cos.at[s, corner_id[d]], cor.at[s, back]))
        return out

    copies = []
    for s in range(STEPS):
        entries = []
        for n, (group, d, src, dst) in enumerate(messages(s)):
            def copy(src=src, dst=dst, s=s, n=n, d=d):
                return pltpu.make_async_remote_copy(
                    src_ref=src, dst_ref=dst,
                    send_sem=send_sem.at[s, n], recv_sem=recv_sem.at[s, n],
                    device_id=device(d), device_id_type=MESH,
                )

            entries.append((group, d, copy))
        copies.append(entries)

    def run(s, groups_wanted, what, backwards=False):
        for d in directions:
            mine = [c for g, e, c in copies[s] if g in groups_wanted and e == d]
            if mine:
                @pl.when(exists[(-d[0], -d[1]) if backwards else d])
                def _(mine=mine):
                    for c in mine:
                        getattr(c(), what)()

    def send(s, *wanted):
        run(s, wanted, "start")

    def receive(s, *wanted):
        run(s, wanted, "wait_recv", backwards=True)

    def pack_y(level, s):
        u, out = (uf, ysf) if level is Fine else (uc, ysc)
        last = 15 if level is Fine else 7
        for side, (j0, j1) in ((LO, (0, 1)), (HI, (last, last - 1))):
            for c in range(3):
                out[s, side, c] = level.plane(u.at[s + 1, c], j0)
            out[s, side, 3] = level.plane(u.at[s + 1, 1], j1)

    def pack_plane(s):
        lane = lanes((8, 128))
        tile = jnp.zeros((8, 128), F32)
        for c in range(3):
            for i in range(8):
                column = uc[s + 1, c, 0, pl.ds(8 * i, 8), 0:1]
                at = 16 * c + 2 * i
                tile = jnp.where((lane == at) | (lane == at + 1), column, tile)
        pls[s] = tile

    def pack_corners(s):
        for (dx, dy), n in corner_id.items():
            fi, fj = (0 if dx < 0 else 15), (0 if dy < 0 else 15)
            ci, cj = (0 if dx < 0 else 7), (0 if dy < 0 else 7)
            rows = []
            for c in (0, 1):
                rows.append(spread_row(uf[s + 1, c, pl.ds(16 * fi + fj, 1), :]))
            for c in (0, 1):
                for h in (0, 1):
                    rows.append(spread_row(uc[s + 1, c, h, pl.ds(8 * ci + cj, 1), :]))
            for j in ((0, 1) if dy < 0 else (7, 7)):
                rows.append(spread_row(pls[s, pl.ds(j, 1), :]))
            sub = subs((8, 128))
            tile = rows[0]
            for m in range(1, 8):
                tile = jnp.where(sub == m, rows[m], tile)
            cos[s, n] = tile

    for dx in (-1, 1):
        @pl.when(jnp.logical_not(exists[(dx, 0)]))
        def _(side=side_of[dx]):
            for s in range(STEPS):
                xhf[s, side] = jnp.zeros(xhf.shape[2:], F32)
                xhc[s, side] = jnp.zeros(xhc.shape[2:], F32)
                plx[s, side] = jnp.zeros((8, 128), F32)
            xmf[side, 0] = jnp.zeros(xmf.shape[2:], F32)
            xmf[side, 1] = jnp.ones(xmf.shape[2:], F32)
            xmc[side, 0] = jnp.zeros(xmc.shape[2:], F32)
            xmc[side, 1] = jnp.ones(xmc.shape[2:], F32)
    for dy in (-1, 1):
        @pl.when(jnp.logical_not(exists[(0, dy)]))
        def _(side=side_of[dy]):
            for s in range(STEPS):
                yhf[s, side] = jnp.zeros(yhf.shape[2:], F32)
                yhc[s, side] = jnp.zeros(yhc.shape[2:], F32)
                ply[s, side] = jnp.zeros((8, 128), F32)
            ymf[side, 0] = jnp.zeros(ymf.shape[2:], F32)
            ymf[side, 1] = jnp.ones(ymf.shape[2:], F32)
            ymc[side, 0] = jnp.zeros(ymc.shape[2:], F32)
            ymc[side, 1] = jnp.ones(ymc.shape[2:], F32)
    for d in corners:
        @pl.when(jnp.logical_not(exists[d]))
        def _(n=corner_id[d]):
            for s in range(STEPS):
                cor[s, n] = jnp.zeros((8, 128), F32)

    wait_load("fine_disp", "coarse_disp", "fine_rigidity", "coarse_rigidity", "fine_metric",
              "coarse_metric")
    for c in (0, 1):
        for side, jf, jc in ((LO, 0, 0), (HI, 15, 7)):
            ysmf[side, c] = Fine.plane(matf.at[c], jf)
            ysmc[side, c] = Coarse.plane(matc.at[c], jc)
    pack_y(Fine, 0)
    pack_y(Coarse, 0)
    pack_plane(0)
    pack_corners(0)

    greeted = n1 - 1 + n2 - 1
    for d in directions:
        greeted = greeted + jnp.where(exists[d], 1, 0).astype(jnp.int32)
    pl.semaphore_wait(barrier, greeted)

    send(0, "co", "cp", "cx", "cy", "mx", "my", "fx", "fy")

    wait_load("fine_density", "fine_lame", "coarse_density", "coarse_lame")
    lane8 = lanes((8, 128))
    spread = jnp.where(
        (lanes((16, 128)) % 16 == subs((16, 128))) & (lanes((16, 128)) < 48), 1.0, 0.0
    ).astype(F32)
    for t in (0, 1):
        pick = jnp.where(lanes((8, 16)) == 2 * subs((8, 16)) + t, 1.0, 0.0).astype(F32)
        for axis in (0, 1):
            table = offsets_ref[axis].astype(F32)
            turned = lax.dot_general(
                pick, table, (((1,), (1,)), ((), ())), preferred_element_type=F32
            )
            shift = jnp.dot(turned, spread, preferred_element_type=F32)
            if axis == 0:
                near = jnp.where(lane8 % 2 == 0, 0.75, 0.25).astype(F32)
            else:
                near = jnp.full((8, 128), 0.75 if t == 0 else 0.25, F32)
            for m, value in enumerate((-1.0, 0.0, 1.0, 2.0)):
                weights[t, 4 * axis + m] = jnp.where(shift == value, near, 0.0) + jnp.where(
                    shift == value - 1.0, 1.0 - near, 0.0
                )

    levels = (
        (Coarse, uc, matc, kc, dvc, dyc, xhc, yhc, ysc, xmc, ymc),
        (Fine, uf, matf, kf, dvf, dyf, xhf, yhf, ysf, xmf, ymf),
    )
    for level, u, mat, k, dv, dy_, xh, yh, ys, xm, ym in levels:
        for i in range(0, level.n, R):
            rig, met, den, lam = (level.load(mat.at[m], i, R) for m in range(4))
            scale = level.edge_scale(rig.shape)
            inverse = 1.0 / met
            light = DT / den
            a = inverse * light
            vertical = rig * inverse
            b = (lam + rig) * light
            isv = inverse * scale
            half_a = 0.5 * a
            for slot, value in (
                (WIDE, rig * met), (HALF_A, half_a), (ISV, isv), (GB, 0.5 * b), (GZ, b * isv),
                (DM, den * met), (CZU, half_a * (vertical + level.k_up(vertical))),
                (CZD, half_a * (vertical + level.k_down(vertical))),
            ):
                level.store(k.at[slot], i, R, value)

    def halo_row(level, ref):
        if level is Fine:
            return Fine.load(ref, 0, 1)
        return Coarse.load(ref, 0, 1)

    def side_coefficients(level, mat, k, xm, ym):
        for i in range(0, level.n, R):
            w = level.load(k.at[WIDE], i, R)
            ha = level.load(k.at[HALF_A], i, R)

            def outer(side):
                return halo_row(level, xm.at[side, 0]) * halo_row(level, xm.at[side, 1])

            cxp = ha * (w + neighbour_rows(level, k.at[WIDE], i, R, 1, lambda: outer(HI)))
            cxm = ha * (w + neighbour_rows(level, k.at[WIDE], i, R, -1, lambda: outer(LO)))
            up = level.row_of(ym.at[HI, 0], i, R) * level.row_of(ym.at[HI, 1], i, R)
            down = level.row_of(ym.at[LO, 0], i, R) * level.row_of(ym.at[LO, 1], i, R)
            cyu = ha * (w + level.j_up(w, up))
            cyd = ha * (w + level.j_down(w, down))
            total = cxp + cxm + cyu + cyd + level.load(k.at[CZU], i, R) + level.load(k.at[CZD], i, R)
            for slot, value in ((CXP, cxp), (CXM, cxm), (CYU, cyu), (CYD, cyd), (C0, total)):
                level.store(k.at[slot], i, R, value)

    def divergences(s, level, u, mat, k, dv, dy_, xh, yh, ys, xm, ym):
        now = u.at[s + 1]
        n = level.n
        for i in range(0, n, R):
            def halo(side):
                return lambda: halo_row(level, xh.at[s, side, 0])

            px = neighbour_rows(level, now.at[0], i, R, 1, halo(HI))
            mx = neighbour_rows(level, now.at[0], i, R, -1, halo(LO))
            y = level.load(now.at[1], i, R)
            z = level.load(now.at[2], i, R)
            py = level.j_up(y, level.row_of(yh.at[s, HI, 1], i, R))
            my = level.j_down(y, level.row_of(yh.at[s, LO, 1], i, R))
            isv = level.load(k.at[ISV], i, R)
            value = 0.5 * ((px - mx) + (py - my)) + isv * (level.k_up(z) - level.k_down(z))
            level.store(dv, i + 1, R, value)
        for dx, side in side_of.items():
            inside = level.load(now.at[0], 0 if dx < 0 else n - 1, 1)
            beyond = halo_row(level, xh.at[s, side, 3])
            y = halo_row(level, xh.at[s, side, 1])
            z = halo_row(level, xh.at[s, side, 2])
            py = level.j_up(y, level.corner_row(cor.at[s, corner_id[(dx, 1)]], 1))
            my = level.j_down(y, level.corner_row(cor.at[s, corner_id[(dx, -1)]], 1))
            isv = level.edge_scale(z.shape) / halo_row(level, xm.at[side, 1])
            along = (beyond - inside) if dx > 0 else (inside - beyond)
            value = 0.5 * (along + (py - my)) + isv * (level.k_up(z) - level.k_down(z))
            level.store(dv, 0 if dx < 0 else n + 1, 1, value * flag((dx, 0)))
        for dy, side in side_of.items():
            x, z, beyond = yh[s, side, 0], yh[s, side, 2], yh[s, side, 3]
            inside = ys[s, side, 1]
            sub = plane_sub(level, x)
            px = jnp.where(sub == n - 1, level.corner_plane(cor.at[s, corner_id[(1, dy)]], 0),
                           plane_roll(level, x, -1))
            mx = jnp.where(sub == 0, level.corner_plane(cor.at[s, corner_id[(-1, dy)]], 0),
                           plane_roll(level, x, 1))
            isv = level.edge_scale(z.shape) / ym[side, 1]
            along = (beyond - inside) if dy > 0 else (inside - beyond)
            value = 0.5 * (along + (px - mx)) + isv * (level.plane_k_up(z) - level.plane_k_down(z))
            dy_[side] = value * flag((0, dy))

    def fine_ghosts(s):
        sub, lane = subs((8, 128)), lanes((8, 128)) % 16

        def shifted_rows(tile, low, high0, high1):
            return [
                jnp.where(sub == 0, low, roll(tile, 1, 0)),
                tile,
                jnp.where(sub == 7, high0, roll(tile, -1, 0)),
                jnp.where(sub == 7, high1, jnp.where(sub == 6, high0, roll(tile, -2, 0))),
            ]

        def row(ref, j):
            return spread_row(ref[pl.ds(j, 1), :])

        def corner_rows(dx):
            low, high = cor.at[s, corner_id[(dx, -1)]], cor.at[s, corner_id[(dx, 1)]]
            return row(low, 6), row(high, 6), row(high, 7)

        own = shifted_rows(pls[s], row(ply.at[s, LO], 7), row(ply.at[s, HI], 0), row(ply.at[s, HI], 1))
        left = shifted_rows(plx[s, LO], *corner_rows(-1))
        right = shifted_rows(plx[s, HI], *corner_rows(1))
        totals = [jnp.zeros((8, 128), F32) for _ in (0, 1)]
        for mx in range(4):
            inner = [jnp.zeros((8, 128), F32) for _ in (0, 1)]
            for my in range(4):
                if mx == 0:
                    tile = jnp.where(lane < 2, roll(left[my], -14, 1), roll(own[my], 2, 1))
                elif mx == 1:
                    tile = own[my]
                elif mx == 2:
                    tile = jnp.where(lane >= 14, roll(right[my], 14, 1), roll(own[my], -2, 1))
                else:
                    tile = jnp.where(lane >= 12, roll(right[my], 12, 1), roll(own[my], -4, 1))
                for t in (0, 1):
                    inner[t] = inner[t] + weights[t, 4 + my] * tile
            for t in (0, 1):
                totals[t] = totals[t] + weights[t, mx] * inner[t]
        for t in (0, 1):
            ghost[t] = totals[t]

    def fine_last(c, i):
        rows = []
        for t in (0, 1):
            tile = ghost[t]
            rows.append(jnp.stack([roll(tile, 127 - (16 * c + i + m), 1) for m in range(R)]))
        return jnp.stack(rows)

    def coarse_first(s, c, i):
        rows = []
        for m in range(R):
            base = 32 * (i + m)
            parts = [uf[s + 1, c, pl.ds(base + t, 8, stride=2), :] for t in (0, 1, 16, 17)]
            rows.append(0.25 * ((parts[0] + parts[1]) + (parts[2] + parts[3])))
        return roll(jnp.stack(rows), 1, 2)

    def rates(s, i, level, u, mat, k, dv, dy_, xh, yh, ys, xm, ym):
        now, old, new = u.at[s + 1], u.at[s], u.at[s + 2]
        coef = {
            m: level.load(k.at[m], i, R) for m in (GB, GZ, DM, CZU, CZD, CXP, CXM, CYU, CYD, C0)
        }
        d_mid = level.load(dv, i + 1, R)
        gradient = [
            coef[GB] * (level.load(dv, i + 2, R) - level.load(dv, i, R)),
            coef[GB]
            * (
                level.j_up(d_mid, level.row_of(dy_.at[HI], i, R))
                - level.j_down(d_mid, level.row_of(dy_.at[LO], i, R))
            ),
            coef[GZ] * (level.k_up(d_mid) - level.k_down(d_mid)),
        ]
        energy = None
        for c in range(3):
            v = level.load(now.at[c], i, R)

            def halo(side, c=c):
                return lambda: halo_row(level, xh.at[s, side, c])

            px = neighbour_rows(level, now.at[c], i, R, 1, halo(HI))
            mx = neighbour_rows(level, now.at[c], i, R, -1, halo(LO))
            py = level.j_up(v, level.row_of(yh.at[s, HI, c], i, R))
            my = level.j_down(v, level.row_of(yh.at[s, LO, c], i, R))
            if level is Fine:
                pz, mz = level.k_up(v, fine_last(c, i)), level.k_down(v)
            else:
                pz = level.k_up(v, jnp.zeros_like(v[1]))
                mz = level.k_down(v, coarse_first(s, c, i))
            rate = (
                (coef[CXP] * px + coef[CXM] * mx)
                + (coef[CYU] * py + coef[CYD] * my)
                + (coef[CZU] * pz + coef[CZD] * mz)
                - coef[C0] * v
                + gradient[c]
            )
            after = (2.0 * v - level.load(old.at[c], i, R)) + rate
            level.store(new.at[c], i, R, after)
            change = after - v
            part = change * change - after * rate
            energy = part if energy is None else energy + part
        return jnp.sum(coef[DM] * energy, axis=(0, 1))

    def order(level):
        n = level.n
        return [0, n - R] + list(range(R, n - R, R))

    coarse_set, fine_set = levels
    for s in range(STEPS):
        last = s == STEPS - 1
        receive(s, "co", "cp", "cx", "cy")
        if s == 0:
            receive(0, "mx", "my")
            side_coefficients(Coarse, matc, kc, xmc, ymc)
            side_coefficients(Fine, matf, kf, xmf, ymf)
            wait_load("fine_prev", "coarse_prev")
        divergences(s, *coarse_set)
        total = jnp.zeros((8, 128), F32)
        for m, i in enumerate(order(Coarse)):
            total = total + rates(s, i, *coarse_set)
            if m == 1 and not last:
                send(s + 1, "cx")
        eacc[s, 1] = total
        if not last:
            pack_y(Coarse, s + 1)
            pack_plane(s + 1)
            send(s + 1, "cy", "cp")
        fine_ghosts(s)
        receive(s, "fx", "fy")
        divergences(s, *fine_set)
        total = jnp.zeros((8, 128), F32)
        for m, i in enumerate(order(Fine)):
            total = total + rates(s, i, *fine_set)
            if m == 1 and not last:
                pack_corners(s + 1)
                send(s + 1, "co", "fx")
        eacc[s, 0] = total
        if not last:
            pack_y(Fine, s + 1)
            send(s + 1, "fy")

    outs = [pltpu.make_async_copy(uf.at[STEPS + 1], fine_out, out_sem.at[0])]
    for h in (0, 1):
        outs.append(
            pltpu.make_async_copy(
                uc.at[STEPS + 1, :, h], coarse_out.at[:, :, pl.ds(128 * h, 128)], out_sem.at[1 + h]
            )
        )
    for c in outs:
        c.start()

    lane1 = lanes((1, 128))
    row = jnp.zeros((1, 128), F32)
    cells = (nx * ny * 16 * 16 * 128, nx * ny * 8 * 8 * 256)
    for s in range(STEPS):
        for m in (0, 1):
            value = jnp.sum(eacc[s, m], axis=0, keepdims=True)
            value = jnp.sum(value, axis=1, keepdims=True)
            row = jnp.where(lane1 == 2 * s + m, value * (1.0 / cells[m]), row)
    erow[0] = row
    er1[me1] = row

    def reduce(n, me, own, buffer, peer, stage):
        def copy(d):
            return pltpu.make_async_remote_copy(
                src_ref=own, dst_ref=buffer.at[me], send_sem=esend.at[stage],
                recv_sem=erecv.at[stage], device_id=peer(d), device_id_type=MESH,
            )

        @pl.loop(1, n)
        def _(d):
            copy(d).start()

        whole = pltpu.make_async_remote_copy(
            src_ref=buffer.at[pl.ds(0, n - 1)], dst_ref=buffer.at[pl.ds(0, n - 1)],
            send_sem=esend.at[stage], recv_sem=erecv.at[stage], device_id=peer(1),
            device_id_type=MESH,
        )
        whole.wait_recv()
        return whole

    done1 = reduce(n1, me1, erow.at[0], er1, peer1, 0)
    row = er1[0]
    for m in range(1, n1):
        row = row + er1[m]
    done2 = None
    if n2 > 1:
        erow[1] = row
        er2[gx_hi] = row
        done2 = reduce(n2, gx_hi, erow.at[1], er2, peer2, 1)
        row = er2[0]
        for m in range(1, n2):
            row = row + er2[m]
    for s in range(STEPS):
        energy_out[pl.ds(s, 1), :] = roll(row, -2 * s, 1)[:, 0:2]

    done1.wait_send()
    if done2 is not None:
        done2.wait_send()
    for s in range(STEPS):
        run(s, ("co", "cp", "cx", "cy", "mx", "my", "fx", "fy"), "wait_send")
    for c in outs:
        c.wait()


def per_device(nx, ny, group_x, *args):
    args = list(args)
    for m in range(4):
        shape = args[m].shape
        args[m] = args[m].reshape(shape[0], shape[1] * shape[2], shape[3])
    for m in range(4, 12):
        shape = args[m].shape
        args[m] = args[m].reshape(shape[0] * shape[1], shape[2])
    vm, dma = pltpu.VMEM, pltpu.SemaphoreType.DMA
    n1, n2 = group_x * ny, nx // group_x
    scratch = [
        vm((STEPS + 2, 3, 256, 128), F32),
        vm((STEPS + 2, 3, 2, 64, 128), F32),
        vm((4, 256, 128), F32),
        vm((4, 2, 64, 128), F32),
        vm((NCOEF, 256, 128), F32),
        vm((NCOEF, 2, 64, 128), F32),
        vm((18 * 16, 128), F32),
        vm((2, 10 * 8, 128), F32),
        vm((2, 16, 128), F32),
        vm((2, 2, 8, 128), F32),
        vm((STEPS, 2, 4, 16, 128), F32),
        vm((STEPS, 2, 4, 2, 8, 128), F32),
        vm((STEPS, 2, 4, 16, 128), F32),
        vm((STEPS, 2, 4, 2, 8, 128), F32),
        vm((STEPS, 2, 4, 16, 128), F32),
        vm((STEPS, 2, 4, 2, 8, 128), F32),
        vm((2, 2, 16, 128), F32),
        vm((2, 2, 2, 8, 128), F32),
        vm((2, 2, 16, 128), F32),
        vm((2, 2, 2, 8, 128), F32),
        vm((2, 2, 16, 128), F32),
        vm((2, 2, 2, 8, 128), F32),
        vm((STEPS, 8, 128), F32),
        vm((STEPS, 2, 8, 128), F32),
        vm((STEPS, 2, 8, 128), F32),
        vm((STEPS, 4, 8, 128), F32),
        vm((STEPS, 4, 8, 128), F32),
        vm((2, 8, 8, 128), F32),
        vm((2, 8, 128), F32),
        vm((STEPS, 2, 8, 128), F32),
        vm((2, 1, 128), F32),
        vm((n1, 1, 128), F32),
        vm((max(n2, 1), 1, 128), F32),
        dma((12, 2)),
        dma((3,)),
        dma((STEPS, 28)),
        dma((STEPS, 28)),
        dma((2,)),
        dma((2,)),
    ]
    anywhere = pl.BlockSpec(memory_space=pltpu.HBM)
    in_vmem = pl.BlockSpec(memory_space=pltpu.VMEM)
    fine, coarse, energy = pl.pallas_call(
        functools.partial(kernel, nx, ny, group_x),
        out_shape=(
            jax.ShapeDtypeStruct((3, 256, 128), F32),
            jax.ShapeDtypeStruct((3, 64, 256), F32),
            jax.ShapeDtypeStruct((STEPS, 2), F32),
        ),
        in_specs=[anywhere] * 12 + [in_vmem],
        out_specs=(anywhere, anywhere, in_vmem),
        scratch_shapes=scratch,
        compiler_params=pltpu.CompilerParams(
            collective_id=0, has_side_effects=True, vmem_limit_bytes=60 << 20
        ),
        name="leapfrog",
    )(*args)
    return fine.reshape(3, 16, 16, 128), coarse.reshape(3, 8, 8, 256), energy


def solution(mesh):
    nx, ny = mesh.shape["gx"], mesh.shape["gy"]
    group_x = 4 if nx % 4 == 0 else 1
    field, cells = P(None, "gx", "gy", None), P("gx", "gy", None)
    return jax.shard_map(
        functools.partial(per_device, nx, ny, group_x),
        mesh=mesh,
        in_specs=(field,) * 4 + (cells,) * 8 + (P(None, "gx", "gy"),),
        out_specs=(field, field, P()),
        check_vma=False,
    )
```

time: 239 us -> 44.6 us (0.19)
  starting transfers between devices: 95.6 us -> 0 us
  blocking collectives: 54.9 us -> 0 us
  Pallas kernels: 0 us -> 39.9 us
  other arithmetic: 39.9 us -> 0 us
  local copies, waits for them, and re-layouts: 39.2 us -> 3.8 us
  between operations: 7.58 us -> 0.65 us
    ppermute x32 -> x0, starting transfers between devices: 95.6 us -> none  [the longest x16 67.2 us: padded(): before = lax.ppermute(last, axis, up)]
    psum x4 -> x0, blocking collectives: 54.9 us -> none  [by_axis(): x = lax.psum(x, axis)]
    pallas_call x0 -> x1, Pallas kernels: none -> 39.9 us  [per_device(): pl.pallas_call(functools.partial(kernel, nx, ny, group_x), out_shape=(jax...]
    mul x44 -> x0, other arithmetic: 17.5 us -> none  [the longest x6 5.73 us: elastic_rate(): flux_z = face_z * (column[:, :, :, 1:] - column[:, :, :, :-1])]
    unnamed x328 -> x7, local copies, waits for them, and re-layouts: 18.2 us -> 3.8 us
    slice x82 -> x0, local copies, waits for them, and re-layouts: 10.6 us -> none  [the longest x60 4.3 us: interpolate(): row_band[:, :, 2 + shift_y:2 + shift_y + coarse_y]]
    another operation x16 -> x0, other arithmetic: 7.2 us -> none  [the longest x12 6.96 us: elastic_rate(): gradient = jnp.stack([grad_x, grad_y, grad_z])]
    mul x19 -> x0, local copies, waits for them, and re-layouts: 7.12 us -> none  [the longest x16 6.48 us: interpolate(): summed = summed + (weight_x * weight_y)[None] * tile_band]
  transfers between devices with their start and end apart: 32 -> 0, of which waited for: 0 -> 0; matrix products, arithmetic and copies ran while one was open for 13% -> 0% of each run, Pallas kernels for 0% -> 0%
where the time goes in v1:
time: 44.6 us; the launch traced here: 44.4 us
  Pallas kernels  39.9 us (89%)
  local copies, waits for them, and re-layouts  3.8 us (9%)
  between operations  0.65 us (1%)
    pallas_call x1, Pallas kernels, per_device(): pl.pallas_call(functools.partial(kernel, nx, ny, group_x), out_shape=(jax...  39.9 us
    unnamed x7, local copies, waits for them, and re-layouts  3.8 us

profile of v1, /device:TPU:1, one launch (start us, length us, event | category | flops | bytes accessed | tf_op | source)
XLA Modules:
  0.0 44.4 jit_solution(577070135723898527)
XLA Ops:
  0.6 39.9 %leapfrog.1 = (f32[3,256,128]{2,1,0:T(8,128)}, f32[3,64,256]{2,1,0:T(8,128)}, f32[3,2]{1,0:T(4,128)}) custom-call(f32[3,256,128]{2,1,0:T(8,128)} %bitcast.15, f32[3,256,128]{2,1,0:T(8,128)} %bitcast.16, f32[3,64,256]{2,1,0:T(8,128)} %bitcast.18, f32[3,64,256]{2,1,0:T(8,128)} %bitcast.19, f32[256,128]{1,0:T(8,128)} %bitcast.20, f32[256,128]{1,0:T(8,128)} %bitcast.21, ...), custom_call_target="tpu_custom_call" | custom-call | tf_op jit(solution)/shard_map/leapfrog/pallas_call | solution.py:804
  40.6 0.0 copy-start.1
  40.6 0.7 %copy-done.1 = f32[3,2]{1,0:T(4,128)S(1)} copy-done((f32[3,2]{1,0:T(4,128)S(1)}, f32[3,2]{1,0:T(4,128)}, u32[]{:S(2)}) %copy-start.1) | copy-done | bytes 48
  41.2 0.6 %copy.16 = f32[3,2]{0,1:T(2,128)} copy(f32[3,2]{1,0:T(4,128)S(1)} %copy-done.1) | data formatting | bytes 48
  41.9 0.0 copy-start
  41.9 1.8 %copy.19 = f32[3,16,16,128]{3,2,1,0:T(8,128)} copy(f32[3,16,16,128]{3,2,1,0:T(8,128)} %bitcast.14) | data formatting | bytes 786432
  43.7 0.0 copy-done
  43.7 0.7 %copy.20 = f32[3,8,8,256]{3,2,1,0:T(8,128)} copy(f32[3,8,8,256]{3,2,1,0:T(8,128)S(1)} %bitcast.17) | data formatting | bytes 393216
Async XLA Ops:
  40.6 0.7 %copy-start.1 = (f32[3,2]{1,0:T(4,128)S(1)}, f32[3,2]{1,0:T(4,128)}, u32[]{:S(2)}) copy-start(f32[3,2]{1,0:T(4,128)} %get-tuple-element.11) | copy-start | bytes 76
  41.9 1.8 %copy-start = (f32[3,64,256]{2,1,0:T(8,128)S(1)}, f32[3,64,256]{2,1,0:T(8,128)}, u32[]{:S(2)}) copy-start(f32[3,64,256]{2,1,0:T(8,128)} %get-tuple-element.7) | copy-start | bytes 589828

commit v2 on v1

--- a/solution.py
+++ b/solution.py
@@ -96,17 +96,13 @@
         return jnp.where(lanes(x.shape) == 0, x, roll(x, 1, 1))
 
     @staticmethod
-    def corner(tile_ref, comp):
-        return spread_row(tile_ref[pl.ds(comp, 1), :])
-
-    @staticmethod
     def corner_plane(tile_ref, comp):
-        row = spread_row(tile_ref[pl.ds(comp, 1), :])
+        row = spread_row(tile_ref[comp])
         return jnp.concatenate([row, row], axis=0)
 
     @staticmethod
     def corner_row(tile_ref, comp):
-        return spread_row(tile_ref[pl.ds(comp, 1), :]).reshape(1, 8, 128)
+        return spread_row(tile_ref[comp]).reshape(1, 8, 128)
 
 
 class Coarse:
@@ -170,11 +166,11 @@
 
     @staticmethod
     def corner_plane(tile_ref, comp):
-        return jnp.stack([spread_row(tile_ref[pl.ds(2 + 2 * comp + h, 1), :]) for h in (0, 1)])
+        return jnp.stack([spread_row(tile_ref[2 * comp + h]) for h in (0, 1)])
 
     @staticmethod
     def corner_row(tile_ref, comp):
-        rows = [spread_row(tile_ref[pl.ds(2 + 2 * comp + h, 1), :]) for h in (0, 1)]
+        rows = [spread_row(tile_ref[2 * comp + h]) for h in (0, 1)]
         return jnp.stack(rows)[:, None]
 
 
@@ -197,18 +193,17 @@
 
 
 def kernel(nx, ny, group_x, *refs):
-    names_in = (
-        "fine_disp fine_prev coarse_disp coarse_prev fine_density fine_lame fine_rigidity"
-        " fine_metric coarse_density coarse_lame coarse_rigidity coarse_metric"
-    ).split()
+    names_in = ["fine_disp", "fine_prev", "coarse_disp", "coarse_prev"]
+    for name in ("fine", "coarse"):
+        names_in += [name + part for part in ("_density", "_lame", "_rigidity", "_metric")]
     hbm = dict(zip(names_in, refs[:12]))
-    offsets_ref = refs[12]
+    offsets_hbm = refs[12]
     fine_out, coarse_out, energy_out = refs[13:16]
     (
         uf, uc, matf, matc, kf, kc, dvf, dvc, dyf, dyc,
         xhf, xhc, yhf, yhc, ysf, ysc, xmf, xmc, ymf, ymc, ysmf, ysmc,
-        pls, plx, ply, cos, cor, weights, ghost, eacc, erow, er1, er2,
-        load_sem, out_sem, send_sem, recv_sem, esend, erecv,
+        pls, plx, ply, pex, ccs, ccr, fcs, fcr, offsets_ref, weights, ghost, eacc, erow, er1, er2,
+        load_sem, send_sem, recv_sem, esend, erecv,
     ) = refs[16:]
 
     gx, gy = lax.axis_index("gx"), lax.axis_index("gy")
@@ -232,32 +227,15 @@
     def device(direction):
         return {"gx": gx + direction[0], "gy": gy + direction[1]}
 
-    groups = nx // group_x
+    groups, half = nx // group_x, ny // 2
     gx_hi, gx_lo = gx // group_x, gx % group_x
+    chip_y, second = gy // 2, gy % 2 == 1
+    first_core = jnp.logical_not(second)
     n1, n2 = group_x * ny, groups
     me1 = gx_lo * ny + gy
-
-    def peer1(d):
-        q = lax.rem(me1 + d, n1)
-        return {"gx": gx_hi * group_x + q // ny, "gy": q % ny}
-
-    def peer2(d):
-        return {"gx": lax.rem(gx_hi + d, n2) * group_x + gx_lo, "gy": gy}
-
-    barrier = pltpu.get_barrier_semaphore()
-    for d in directions:
-        @pl.when(exists[d])
-        def _(d=d):
-            pl.semaphore_signal(barrier, inc=1, device_id=device(d), device_id_type=MESH)
-
-    @pl.loop(1, n1)
-    def _(d):
-        pl.semaphore_signal(barrier, inc=1, device_id=peer1(d), device_id_type=MESH)
-
-    if n2 > 1:
-        @pl.loop(1, n2)
-        def _(d):
-            pl.semaphore_signal(barrier, inc=1, device_id=peer2(d), device_id_type=MESH)
+    plane_x = [gx_hi * group_x + lax.rem(gx_lo + a, group_x) for a in range(group_x)]
+    plane_y = [2 * lax.rem(chip_y + b, half) for b in range(half)]
+    line_x = [lax.rem(gx_hi + d, n2) * group_x + gx_lo for d in range(n2)]
 
     loads = {}
 
@@ -291,10 +269,39 @@
     for sem, (name, dst) in enumerate(plan):
         start_load(name, dst, sem)
 
+    loads["offsets"] = [pltpu.make_async_copy(offsets_hbm, offsets_ref, load_sem.at[12, 0])]
+    loads["offsets"][0].start()
+
     def wait_load(*names):
         for name in names:
             for c in loads[name]:
                 c.wait()
+
+    barrier = pltpu.get_barrier_semaphore()
+
+    def greet(where):
+        pl.semaphore_signal(barrier, inc=1, device_id=where, device_id_type=MESH)
+
+    far_first = sorted(range(1, n2), key=lambda d: -min(d, n2 - d))
+    for d in far_first:
+        greet({"gx": line_x[d], "gy": 2 * chip_y + 1})
+    for d in directions:
+        @pl.when(exists[d])
+        def _(d=d):
+            greet(device(d))
+
+    @pl.when(first_core)
+    def _():
+        greet({"gx": gx, "gy": 2 * chip_y + 1})
+
+    @pl.when(second)
+    def _():
+        for x in plane_x:
+            for y in plane_y:
+                if not (x is plane_x[0] and y is plane_y[0]):
+                    greet({"gx": x, "gy": y})
+                    greet({"gx": x, "gy": y + 1})
+        greet({"gx": gx, "gy": 2 * chip_y})
 
     side_of = {-1: LO, 1: HI}
 
@@ -309,23 +316,24 @@
             first, second = (0, 1) if dx < 0 else (7, 6)
             out.append(("cx", (dx, 0), u_c.at[:, :, pl.ds(8 * first, 8)], xhc.at[s, far, pl.ds(0, 3)]))
             out.append(("cx", (dx, 0), u_c.at[0, :, pl.ds(8 * second, 8)], xhc.at[s, far, 3]))
-            out.append(("cp", (dx, 0), pls.at[s], plx.at[s, far]))
+            out.append(("cp", (dx, 0), pex.at[s], plx.at[s, far]))
             if s == 0:
                 first = 0 if dx < 0 else 15
-                out.append(("mx", (dx, 0), matf.at[pl.ds(0, 2), pl.ds(16 * first, 16)], xmf.at[far]))
+                out.append(("mf", (dx, 0), matf.at[pl.ds(0, 2), pl.ds(16 * first, 16)], xmf.at[far]))
                 first = 0 if dx < 0 else 7
-                out.append(("mx", (dx, 0), matc.at[pl.ds(0, 2), :, pl.ds(8 * first, 8)], xmc.at[far]))
+                out.append(("mc", (dx, 0), matc.at[pl.ds(0, 2), :, pl.ds(8 * first, 8)], xmc.at[far]))
         for dy in (-1, 1):
             own, far = side_of[dy], side_of[-dy]
             out.append(("fy", (0, dy), ysf.at[s, own], yhf.at[s, far]))
             out.append(("cy", (0, dy), ysc.at[s, own], yhc.at[s, far]))
-            out.append(("cp", (0, dy), pls.at[s], ply.at[s, far]))
+            out.append(("cq", (0, dy), pls.at[s], ply.at[s, far]))
             if s == 0:
-                out.append(("my", (0, dy), ysmf.at[own], ymf.at[far]))
-                out.append(("my", (0, dy), ysmc.at[own], ymc.at[far]))
+                out.append(("mf", (0, dy), ysmf.at[own], ymf.at[far]))
+                out.append(("mc", (0, dy), ysmc.at[own], ymc.at[far]))
         for d in corners:
             back = corner_id[(-d[0], -d[1])]
-            out.append(("co", d, cos.at[s, corner_id[d]], cor.at[s, back]))
+            out.append(("co", d, ccs.at[s, corner_id[d]], ccr.at[s, back]))
+            out.append(("fo", d, fcs.at[s, corner_id[d]], fcr.at[s, back]))
         return out
 
     copies = []
@@ -365,33 +373,33 @@
                 out[s, side, c] = level.plane(u.at[s + 1, c], j0)
             out[s, side, 3] = level.plane(u.at[s + 1, 1], j1)
 
-    def pack_plane(s):
+    def plane_tile(s, tile, rows):
         lane = lanes((8, 128))
-        tile = jnp.zeros((8, 128), F32)
         for c in range(3):
-            for i in range(8):
+            for i in rows:
                 column = uc[s + 1, c, 0, pl.ds(8 * i, 8), 0:1]
                 at = 16 * c + 2 * i
                 tile = jnp.where((lane == at) | (lane == at + 1), column, tile)
-        pls[s] = tile
+        return tile
+
+    def pack_edge(s):
+        pex[s] = plane_tile(s, jnp.zeros((8, 128), F32), (0, 1, 7))
+        for (dx, dy), n in corner_id.items():
+            ci, cj = (0 if dx < 0 else 7), (0 if dy < 0 else 7)
+            for c in (0, 1):
+                for h in (0, 1):
+                    ccs[s, n, 2 * c + h] = uc[s + 1, c, h, pl.ds(8 * ci + cj, 1), :]
+            for m, j in enumerate((0, 1) if dy < 0 else (7, 7)):
+                ccs[s, n, 4 + m] = pex[s, pl.ds(j, 1), :]
+
+    def pack_plane(s):
+        pls[s] = plane_tile(s, pex[s], range(2, 7))
 
     def pack_corners(s):
         for (dx, dy), n in corner_id.items():
             fi, fj = (0 if dx < 0 else 15), (0 if dy < 0 else 15)
-            ci, cj = (0 if dx < 0 else 7), (0 if dy < 0 else 7)
-            rows = []
             for c in (0, 1):
-                rows.append(spread_row(uf[s + 1, c, pl.ds(16 * fi + fj, 1), :]))
-            for c in (0, 1):
-                for h in (0, 1):
-                    rows.append(spread_row(uc[s + 1, c, h, pl.ds(8 * ci + cj, 1), :]))
-            for j in ((0, 1) if dy < 0 else (7, 7)):
-                rows.append(spread_row(pls[s, pl.ds(j, 1), :]))
-            sub = subs((8, 128))
-            tile = rows[0]
-            for m in range(1, 8):
-                tile = jnp.where(sub == m, rows[m], tile)
-            cos[s, n] = tile
+                fcs[s, n, c] = uf[s + 1, c, pl.ds(16 * fi + fj, 1), :]
 
     for dx in (-1, 1):
         @pl.when(jnp.logical_not(exists[(dx, 0)]))
@@ -419,7 +427,8 @@
         @pl.when(jnp.logical_not(exists[d]))
         def _(n=corner_id[d]):
             for s in range(STEPS):
-                cor[s, n] = jnp.zeros((8, 128), F32)
+                ccr[s, n] = jnp.zeros(ccr.shape[2:], F32)
+                fcr[s, n] = jnp.zeros(fcr.shape[2:], F32)
 
     wait_load("fine_disp", "coarse_disp", "fine_rigidity", "coarse_rigidity", "fine_metric",
               "coarse_metric")
@@ -429,17 +438,20 @@
             ysmc[side, c] = Coarse.plane(matc.at[c], jc)
     pack_y(Fine, 0)
     pack_y(Coarse, 0)
+    pack_edge(0)
     pack_plane(0)
     pack_corners(0)
 
-    greeted = n1 - 1 + n2 - 1
+    greeted = jnp.where(second, n1 // 2 - 1 + 2 * (n2 - 1) + 1, n1 // 2).astype(jnp.int32)
     for d in directions:
         greeted = greeted + jnp.where(exists[d], 1, 0).astype(jnp.int32)
     pl.semaphore_wait(barrier, greeted)
 
-    send(0, "co", "cp", "cx", "cy", "mx", "my", "fx", "fy")
-
-    wait_load("fine_density", "fine_lame", "coarse_density", "coarse_lame")
+    send(0, "cx", "cy", "mc", "co", "cp", "cq")
+    send(0, "fo", "mf")
+    send(0, "fx", "fy")
+
+    wait_load("fine_density", "fine_lame", "coarse_density", "coarse_lame", "offsets")
     lane8 = lanes((8, 128))
     spread = jnp.where(
         (lanes((16, 128)) % 16 == subs((16, 128))) & (lanes((16, 128)) < 48), 1.0, 0.0
@@ -507,6 +519,7 @@
                 level.store(k.at[slot], i, R, value)
 
     def divergences(s, level, u, mat, k, dv, dy_, xh, yh, ys, xm, ym):
+        cor = fcr if level is Fine else ccr
         now = u.at[s + 1]
         n = level.n
         for i in range(0, n, R):
@@ -561,8 +574,8 @@
             return spread_row(ref[pl.ds(j, 1), :])
 
         def corner_rows(dx):
-            low, high = cor.at[s, corner_id[(dx, -1)]], cor.at[s, corner_id[(dx, 1)]]
-            return row(low, 6), row(high, 6), row(high, 7)
+            low, high = ccr.at[s, corner_id[(dx, -1)]], ccr.at[s, corner_id[(dx, 1)]]
+            return spread_row(low[4]), spread_row(high[4]), spread_row(high[5])
 
         own = shifted_rows(pls[s], row(ply.at[s, LO], 7), row(ply.at[s, HI], 0), row(ply.at[s, HI], 1))
         left = shifted_rows(plx[s, LO], *corner_rows(-1))
@@ -602,7 +615,7 @@
         return roll(jnp.stack(rows), 1, 2)
 
     def rates(s, i, level, u, mat, k, dv, dy_, xh, yh, ys, xm, ym):
-        now, old, new = u.at[s + 1], u.at[s], u.at[s + 2]
+        now, old = u.at[s + 1], u.at[s]
         coef = {
             m: level.load(k.at[m], i, R) for m in (GB, GZ, DM, CZU, CZD, CXP, CXM, CYU, CYD, C0)
         }
@@ -640,7 +653,15 @@
                 + gradient[c]
             )
             after = (2.0 * v - level.load(old.at[c], i, R)) + rate
-            level.store(new.at[c], i, R, after)
+            if s < STEPS - 1:
+                level.store(u.at[s + 2, c], i, R, after)
+            elif level is Fine:
+                level.store(fine_out.at[c], i, R, after)
+            else:
+                for h in (0, 1):
+                    coarse_out[c, pl.ds(8 * i, 8 * R), pl.ds(128 * h, 128)] = after[h].reshape(
+                        8 * R, 128
+                    )
             change = after - v
             part = change * change - after * rate
             energy = part if energy is None else energy + part
@@ -653,46 +674,41 @@
     coarse_set, fine_set = levels
     for s in range(STEPS):
         last = s == STEPS - 1
-        receive(s, "co", "cp", "cx", "cy")
+        receive(s, "cx", "cy", "co")
         if s == 0:
-            receive(0, "mx", "my")
+            receive(0, "mc")
             side_coefficients(Coarse, matc, kc, xmc, ymc)
-            side_coefficients(Fine, matf, kf, xmf, ymf)
-            wait_load("fine_prev", "coarse_prev")
+            wait_load("coarse_prev")
         divergences(s, *coarse_set)
         total = jnp.zeros((8, 128), F32)
         for m, i in enumerate(order(Coarse)):
             total = total + rates(s, i, *coarse_set)
             if m == 1 and not last:
-                send(s + 1, "cx")
+                pack_edge(s + 1)
+                send(s + 1, "cx", "co", "cp")
         eacc[s, 1] = total
         if not last:
             pack_y(Coarse, s + 1)
             pack_plane(s + 1)
-            send(s + 1, "cy", "cp")
+            send(s + 1, "cy", "cq")
+        receive(s, "cp", "cq")
         fine_ghosts(s)
-        receive(s, "fx", "fy")
+        receive(s, "fx", "fy", "fo")
+        if s == 0:
+            receive(0, "mf")
+            side_coefficients(Fine, matf, kf, xmf, ymf)
+            wait_load("fine_prev")
         divergences(s, *fine_set)
         total = jnp.zeros((8, 128), F32)
         for m, i in enumerate(order(Fine)):
             total = total + rates(s, i, *fine_set)
             if m == 1 and not last:
                 pack_corners(s + 1)
-                send(s + 1, "co", "fx")
+                send(s + 1, "fo", "fx")
         eacc[s, 0] = total
         if not last:
             pack_y(Fine, s + 1)
             send(s + 1, "fy")
-
-    outs = [pltpu.make_async_copy(uf.at[STEPS + 1], fine_out, out_sem.at[0])]
-    for h in (0, 1):
-        outs.append(
-            pltpu.make_async_copy(
-                uc.at[STEPS + 1, :, h], coarse_out.at[:, :, pl.ds(128 * h, 128)], out_sem.at[1 + h]
-            )
-        )
-    for c in outs:
-        c.start()
 
     lane1 = lanes((1, 128))
     row = jnp.zeros((1, 128), F32)
@@ -701,50 +717,75 @@
         for m in (0, 1):
             value = jnp.sum(eacc[s, m], axis=0, keepdims=True)
             value = jnp.sum(value, axis=1, keepdims=True)
-            row = jnp.where(lane1 == 2 * s + m, value * (1.0 / cells[m]), row)
+            row = jnp.where(lane1 == STEPS * m + s, value * (1.0 / cells[m]), row)
     erow[0] = row
     er1[me1] = row
 
-    def reduce(n, me, own, buffer, peer, stage):
-        def copy(d):
-            return pltpu.make_async_remote_copy(
-                src_ref=own, dst_ref=buffer.at[me], send_sem=esend.at[stage],
-                recv_sem=erecv.at[stage], device_id=peer(d), device_id_type=MESH,
-            )
-
-        @pl.loop(1, n)
-        def _(d):
-            copy(d).start()
-
-        whole = pltpu.make_async_remote_copy(
-            src_ref=buffer.at[pl.ds(0, n - 1)], dst_ref=buffer.at[pl.ds(0, n - 1)],
-            send_sem=esend.at[stage], recv_sem=erecv.at[stage], device_id=peer(1),
-            device_id_type=MESH,
+    def rows(buffer, n, stage):
+        part = buffer.at[pl.ds(0, n)]
+        return pltpu.make_async_remote_copy(
+            src_ref=part, dst_ref=part, send_sem=esend.at[stage], recv_sem=erecv.at[stage],
+            device_id={"gx": line_x[0], "gy": gy}, device_id_type=MESH,
         )
-        whole.wait_recv()
-        return whole
-
-    done1 = reduce(n1, me1, erow.at[0], er1, peer1, 0)
-    row = er1[0]
-    for m in range(1, n1):
-        row = row + er1[m]
-    done2 = None
-    if n2 > 1:
-        erow[1] = row
-        er2[gx_hi] = row
-        done2 = reduce(n2, gx_hi, erow.at[1], er2, peer2, 1)
-        row = er2[0]
-        for m in range(1, n2):
-            row = row + er2[m]
+
+    def pass_on(stage, slot, where):
+        pltpu.make_async_remote_copy(
+            src_ref=erow.at[stage], dst_ref=slot, send_sem=esend.at[stage],
+            recv_sem=erecv.at[stage], device_id=where, device_id_type=MESH,
+        ).start()
+
+    for a in reversed(range(group_x)):
+        for b in reversed(range(half)):
+            if a or b:
+                pass_on(0, er1.at[me1], {"gx": plane_x[a], "gy": plane_y[b] + 1})
+
+    @pl.when(first_core)
+    def _():
+        pass_on(0, er1.at[me1], {"gx": gx, "gy": 2 * chip_y + 1})
+
+    @pl.when(second)
+    def _():
+        rows(er1, n1 - 1, 0).wait_recv()
+        plane = er1[0]
+        for m in range(1, n1):
+            plane = plane + er1[m]
+        erow[1] = plane
+        er2[gx_hi] = plane
+        for d in far_first:
+            for core in (0, 1):
+                pass_on(1, er2.at[gx_hi], {"gx": line_x[d], "gy": 2 * chip_y + core})
+        pass_on(1, er2.at[gx_hi], {"gx": gx, "gy": 2 * chip_y})
+        if n2 > 1:
+            rows(er2, n2 - 1, 1).wait_recv()
+
+    @pl.when(first_core)
+    def _():
+        rows(er2, n2, 1).wait_recv()
+
+    row = er2[0]
+    for m in range(1, n2):
+        row = row + er2[m]
+    for m in (0, 1):
+        energy_out[pl.ds(m, 1), :] = roll(row, -STEPS * m, 1)[:, 0:STEPS]
+
+    @pl.when(second)
+    def _():
+        rows(er1, n1 // 2 - 1, 0).wait_send()
+        rows(er1, 2 * n2 - 1, 1).wait_send()
+
+    @pl.when(first_core)
+    def _():
+        rows(er1, n1 // 2, 0).wait_send()
+
     for s in range(STEPS):
-        energy_out[pl.ds(s, 1), :] = roll(row, -2 * s, 1)[:, 0:2]
-
-    done1.wait_send()
-    if done2 is not None:
-        done2.wait_send()
-    for s in range(STEPS):
-        run(s, ("co", "cp", "cx", "cy", "mx", "my", "fx", "fy"), "wait_send")
-    for c in outs:
+        run(s, ("co", "cp", "cq", "fo", "cx", "cy", "mc", "mf", "fx", "fy"), "wait_send")
+
+
+def hand_out(*refs):
+    copies = [pltpu.make_async_copy(refs[n], refs[3 + n], refs[6].at[n]) for n in range(3)]
+    for c in copies:
+        c.start()
+    for c in copies:
         c.wait()
 
 
@@ -756,11 +797,13 @@
     for m in range(4, 12):
         shape = args[m].shape
         args[m] = args[m].reshape(shape[0] * shape[1], shape[2])
+    for m in range(13):
+        args[m] = pltpu.with_memory_space_constraint(args[m], pltpu.HBM)
     vm, dma = pltpu.VMEM, pltpu.SemaphoreType.DMA
     n1, n2 = group_x * ny, nx // group_x
     scratch = [
-        vm((STEPS + 2, 3, 256, 128), F32),
-        vm((STEPS + 2, 3, 2, 64, 128), F32),
+        vm((STEPS + 1, 3, 256, 128), F32),
+        vm((STEPS + 1, 3, 2, 64, 128), F32),
         vm((4, 256, 128), F32),
         vm((4, 2, 64, 128), F32),
         vm((NCOEF, 256, 128), F32),
@@ -784,44 +827,58 @@
         vm((STEPS, 8, 128), F32),
         vm((STEPS, 2, 8, 128), F32),
         vm((STEPS, 2, 8, 128), F32),
-        vm((STEPS, 4, 8, 128), F32),
-        vm((STEPS, 4, 8, 128), F32),
+        vm((STEPS, 8, 128), F32),
+        vm((STEPS, 4, 6, 1, 128), F32),
+        vm((STEPS, 4, 6, 1, 128), F32),
+        vm((STEPS, 4, 2, 1, 128), F32),
+        vm((STEPS, 4, 2, 1, 128), F32),
+        vm((2, 16, 16), jnp.int32),
         vm((2, 8, 8, 128), F32),
         vm((2, 8, 128), F32),
         vm((STEPS, 2, 8, 128), F32),
         vm((2, 1, 128), F32),
-        vm((n1, 1, 128), F32),
+        vm((max(n1, 2 * n2), 1, 128), F32),
         vm((max(n2, 1), 1, 128), F32),
-        dma((12, 2)),
-        dma((3,)),
-        dma((STEPS, 28)),
-        dma((STEPS, 28)),
+        dma((13, 2)),
+        dma((STEPS, 32)),
+        dma((STEPS, 32)),
         dma((2,)),
         dma((2,)),
     ]
     anywhere = pl.BlockSpec(memory_space=pltpu.HBM)
     in_vmem = pl.BlockSpec(memory_space=pltpu.VMEM)
-    fine, coarse, energy = pl.pallas_call(
+    out_shape = (
+        jax.ShapeDtypeStruct((3, 256, 128), F32),
+        jax.ShapeDtypeStruct((3, 64, 256), F32),
+        jax.ShapeDtypeStruct((2, STEPS), F32),
+    )
+    results = pl.pallas_call(
         functools.partial(kernel, nx, ny, group_x),
-        out_shape=(
-            jax.ShapeDtypeStruct((3, 256, 128), F32),
-            jax.ShapeDtypeStruct((3, 64, 256), F32),
-            jax.ShapeDtypeStruct((STEPS, 2), F32),
-        ),
-        in_specs=[anywhere] * 12 + [in_vmem],
-        out_specs=(anywhere, anywhere, in_vmem),
+        out_shape=out_shape,
+        in_specs=[anywhere] * 13,
+        out_specs=(in_vmem, in_vmem, in_vmem),
         scratch_shapes=scratch,
         compiler_params=pltpu.CompilerParams(
-            collective_id=0, has_side_effects=True, vmem_limit_bytes=60 << 20
+            collective_id=0, has_side_effects=True, vmem_limit_bytes=32 << 20
         ),
         name="leapfrog",
     )(*args)
+    fine, coarse, energy = pl.pallas_call(
+        hand_out,
+        out_shape=out_shape,
+        in_specs=[in_vmem] * 3,
+        out_specs=[anywhere] * 3,
+        scratch_shapes=[dma((3,))],
+        compiler_params=pltpu.CompilerParams(vmem_limit_bytes=1 << 20),
+        name="hand_out",
+    )(*results)
+    energy = energy.T
     return fine.reshape(3, 16, 16, 128), coarse.reshape(3, 8, 8, 256), energy
 
 
 def solution(mesh):
     nx, ny = mesh.shape["gx"], mesh.shape["gy"]
-    group_x = 4 if nx % 4 == 0 else 1
+    group_x = next(m for m in (4, 2, 1) if nx % m == 0)
     field, cells = P(None, "gx", "gy", None), P("gx", "gy", None)
     return jax.shard_map(
         functools.partial(per_device, nx, ny, group_x),

time: 44.6 us -> 38.3 us (0.86)
  local copies, waits for them, and re-layouts: 3.8 us -> 0 us
  Pallas kernels: 39.9 us -> 37.6 us
    unnamed x7 -> x0, local copies, waits for them, and re-layouts: 3.8 us -> none
    pallas_call x1 -> x2, Pallas kernels: 39.9 us -> 37.6 us  [the longest x1 36.8 us: per_device(): pl.pallas_call(functools.partial(kernel, nx, ny, group_x), out_shape=out_...]
where the time goes in v2:
time: 38.3 us; the launch traced here: 38.2 us
  Pallas kernels  37.6 us (98%)
  between operations  0.64 us (2%)
    pallas_call x1, Pallas kernels, per_device(): pl.pallas_call(functools.partial(kernel, nx, ny, group_x), out_shape=out_...  36.8 us
    pallas_call x1, Pallas kernels, per_device(): pl.pallas_call(hand_out, out_shape=out_shape, in_specs=[in_vmem] * 3, out...  0.84 us

profile of v2, /device:TPU:1, one launch (start us, length us, event | category | flops | bytes accessed | tf_op | source)
XLA Modules:
  0.0 38.2 jit_solution(6087259966213043913)
XLA Ops:
  0.6 36.8 %leapfrog.1 = (f32[3,256,128]{2,1,0:T(8,128)S(1)}, f32[3,64,256]{2,1,0:T(8,128)S(1)}, f32[2,3]{1,0:T(2,128)S(1)}) custom-call(f32[3,256,128]{2,1,0:T(8,128)} %bitcast.15, f32[3,256,128]{2,1,0:T(8,128)} %bitcast.16, f32[3,64,256]{2,1,0:T(8,128)} %bitcast.17, f32[3,64,256]{2,1,0:T(8,128)} %bitcast.18, f32[256,128]{1,0:T(8,128)} %bitcast.19, ...), custom_call_target="tpu_custom_call" | custom-call | tf_op jit(solution)/shard_map/leapfrog/pallas_call | solution.py:855
  37.4 0.8 %hand_out.1 = (f32[3,256,128]{2,1,0:T(8,128)}, f32[3,64,256]{2,1,0:T(8,128)}, f32[2,3]{1,0:T(2,128)}) custom-call(f32[3,256,128]{2,1,0:T(8,128)S(1)} %get-tuple-element.9.refs_0_, f32[3,64,256]{2,1,0:T(8,128)S(1)} %get-tuple-element.10.refs_1_, f32[2,3]{1,0:T(2,128)S(1)} %get-tuple-element.11.refs_2_), custom_call_target="tpu_custom_call" | custom-call | tf_op jit(solution)/shard_map/hand_out/pallas_call | solution.py:866

commit v3 on v2

--- a/solution.py
+++ b/solution.py
@@ -186,10 +186,10 @@
     if step > 0:
         if i + r < level.n:
             return level.load(ref, i + 1, r)
-        return jnp.concatenate([level.load(ref, i + 1, r - 1), halo()], axis=1)
+        return halo() if r == 1 else jnp.concatenate([level.load(ref, i + 1, r - 1), halo()], axis=1)
     if i > 0:
         return level.load(ref, i - 1, r)
-    return jnp.concatenate([halo(), level.load(ref, 0, r - 1)], axis=1)
+    return halo() if r == 1 else jnp.concatenate([halo(), level.load(ref, 0, r - 1)], axis=1)
 
 
 def kernel(nx, ny, group_x, *refs):
@@ -202,8 +202,8 @@
     (
         uf, uc, matf, matc, kf, kc, dvf, dvc, dyf, dyc,
         xhf, xhc, yhf, yhc, ysf, ysc, xmf, xmc, ymf, ymc, ysmf, ysmc,
-        pls, plx, ply, pex, ccs, ccr, fcs, fcr, offsets_ref, weights, ghost, eacc, erow, er1, er2,
-        load_sem, send_sem, recv_sem, esend, erecv,
+        pls, plx, ply, pex, ccs, ccr, cps, cpr, fcs, fcr, offsets_ref, weights, ghost, eacc, erow, er1, er2,
+        load_sem, send_sem, recv_sem, esend, erecv, line_sem,
     ) = refs[16:]
 
     gx, gy = lax.axis_index("gx"), lax.axis_index("gy")
@@ -213,9 +213,7 @@
             ([gx > 0] if dx < 0 else [gx < nx - 1] if dx > 0 else [])
             + ([gy > 0] if dy < 0 else [gy < ny - 1] if dy > 0 else []),
         )
-        for dx in (-1, 0, 1)
-        for dy in (-1, 0, 1)
-        if (dx, dy) != (0, 0)
+        for dx, dy in ((-1, 0), (1, 0), (-1, -1), (-1, 1), (1, -1), (1, 1), (0, -1), (0, 1))
     }
     directions = list(exists)
     corners = [d for d in directions if d[0] and d[1]]
@@ -283,7 +281,9 @@
         pl.semaphore_signal(barrier, inc=1, device_id=where, device_id_type=MESH)
 
     far_first = sorted(range(1, n2), key=lambda d: -min(d, n2 - d))
-    for d in far_first:
+    by_one = sorted({1, n2 - 1}) if n2 > 1 else []
+    by_two = sorted({2, n2 - 2}) if n2 > 3 else []
+    for d in by_one:
         greet({"gx": line_x[d], "gy": 2 * chip_y + 1})
     for d in directions:
         @pl.when(exists[d])
@@ -333,6 +333,7 @@
         for d in corners:
             back = corner_id[(-d[0], -d[1])]
             out.append(("co", d, ccs.at[s, corner_id[d]], ccr.at[s, back]))
+            out.append(("cp", d, cps.at[s, corner_id[d]], cpr.at[s, back]))
             out.append(("fo", d, fcs.at[s, corner_id[d]], fcr.at[s, back]))
         return out
 
@@ -365,6 +366,21 @@
     def receive(s, *wanted):
         run(s, wanted, "wait_recv", backwards=True)
 
+    def line_round(stage):
+        steps = (by_one, by_two)[stage] if n2 > 3 else []
+
+        @pl.when(second)
+        def _():
+            for m, d in enumerate(steps):
+                pl.semaphore_signal(
+                    line_sem.at[stage, m], inc=1,
+                    device_id={"gx": line_x[d], "gy": gy}, device_id_type=MESH,
+                )
+
+    def line_wait(stage):
+        for m in range(len((by_one, by_two)[stage]) if n2 > 3 else 0):
+            pl.semaphore_wait(line_sem.at[stage, m], 1)
+
     def pack_y(level, s):
         u, out = (uf, ysf) if level is Fine else (uc, ysc)
         last = 15 if level is Fine else 7
@@ -382,18 +398,20 @@
                 tile = jnp.where((lane == at) | (lane == at + 1), column, tile)
         return tile
 
-    def pack_edge(s):
-        pex[s] = plane_tile(s, jnp.zeros((8, 128), F32), (0, 1, 7))
+    def pack_coarse_corners(s):
         for (dx, dy), n in corner_id.items():
             ci, cj = (0 if dx < 0 else 7), (0 if dy < 0 else 7)
             for c in (0, 1):
                 for h in (0, 1):
                     ccs[s, n, 2 * c + h] = uc[s + 1, c, h, pl.ds(8 * ci + cj, 1), :]
+
+    def pack_plane(s):
+        edge = plane_tile(s, jnp.zeros((8, 128), F32), (0, 1, 7))
+        pex[s] = edge
+        pls[s] = plane_tile(s, edge, range(2, 7))
+        for (dx, dy), n in corner_id.items():
             for m, j in enumerate((0, 1) if dy < 0 else (7, 7)):
-                ccs[s, n, 4 + m] = pex[s, pl.ds(j, 1), :]
-
-    def pack_plane(s):
-        pls[s] = plane_tile(s, pex[s], range(2, 7))
+                cps[s, n, m] = edge[j : j + 1]
 
     def pack_corners(s):
         for (dx, dy), n in corner_id.items():
@@ -428,6 +446,7 @@
         def _(n=corner_id[d]):
             for s in range(STEPS):
                 ccr[s, n] = jnp.zeros(ccr.shape[2:], F32)
+                cpr[s, n] = jnp.zeros(cpr.shape[2:], F32)
                 fcr[s, n] = jnp.zeros(fcr.shape[2:], F32)
 
     wait_load("fine_disp", "coarse_disp", "fine_rigidity", "coarse_rigidity", "fine_metric",
@@ -438,18 +457,19 @@
             ysmc[side, c] = Coarse.plane(matc.at[c], jc)
     pack_y(Fine, 0)
     pack_y(Coarse, 0)
-    pack_edge(0)
+    pack_coarse_corners(0)
     pack_plane(0)
     pack_corners(0)
 
-    greeted = jnp.where(second, n1 // 2 - 1 + 2 * (n2 - 1) + 1, n1 // 2).astype(jnp.int32)
+    greeted = jnp.where(second, n1 // 2 + 2 * len(by_one), n1 // 2).astype(jnp.int32)
     for d in directions:
         greeted = greeted + jnp.where(exists[d], 1, 0).astype(jnp.int32)
     pl.semaphore_wait(barrier, greeted)
 
-    send(0, "cx", "cy", "mc", "co", "cp", "cq")
-    send(0, "fo", "mf")
-    send(0, "fx", "fy")
+    send(0, "co")
+    send(0, "cx", "cy", "mc")
+    send(0, "fo", "fx", "fy", "mf")
+    send(0, "cp", "cq")
 
     wait_load("fine_density", "fine_lame", "coarse_density", "coarse_lame", "offsets")
     lane8 = lanes((8, 128))
@@ -518,23 +538,25 @@
             for slot, value in ((CXP, cxp), (CXM, cxm), (CYU, cyu), (CYD, cyd), (C0, total)):
                 level.store(k.at[slot], i, R, value)
 
-    def divergences(s, level, u, mat, k, dv, dy_, xh, yh, ys, xm, ym):
+    def row_divergence(s, i, r, level, u, mat, k, dv, dy_, xh, yh, ys, xm, ym):
+        now = u.at[s + 1]
+
+        def halo(side):
+            return lambda: halo_row(level, xh.at[s, side, 0])
+
+        px = neighbour_rows(level, now.at[0], i, r, 1, halo(HI))
+        mx = neighbour_rows(level, now.at[0], i, r, -1, halo(LO))
+        y = level.load(now.at[1], i, r)
+        z = level.load(now.at[2], i, r)
+        py = level.j_up(y, level.row_of(yh.at[s, HI, 1], i, r))
+        my = level.j_down(y, level.row_of(yh.at[s, LO, 1], i, r))
+        isv = level.load(k.at[ISV], i, r)
+        value = 0.5 * ((px - mx) + (py - my)) + isv * (level.k_up(z) - level.k_down(z))
+        level.store(dv, i + 1, r, value)
+
+    def x_side_divergence(s, level, u, mat, k, dv, dy_, xh, yh, ys, xm, ym):
         cor = fcr if level is Fine else ccr
-        now = u.at[s + 1]
-        n = level.n
-        for i in range(0, n, R):
-            def halo(side):
-                return lambda: halo_row(level, xh.at[s, side, 0])
-
-            px = neighbour_rows(level, now.at[0], i, R, 1, halo(HI))
-            mx = neighbour_rows(level, now.at[0], i, R, -1, halo(LO))
-            y = level.load(now.at[1], i, R)
-            z = level.load(now.at[2], i, R)
-            py = level.j_up(y, level.row_of(yh.at[s, HI, 1], i, R))
-            my = level.j_down(y, level.row_of(yh.at[s, LO, 1], i, R))
-            isv = level.load(k.at[ISV], i, R)
-            value = 0.5 * ((px - mx) + (py - my)) + isv * (level.k_up(z) - level.k_down(z))
-            level.store(dv, i + 1, R, value)
+        now, n = u.at[s + 1], level.n
         for dx, side in side_of.items():
             inside = level.load(now.at[0], 0 if dx < 0 else n - 1, 1)
             beyond = halo_row(level, xh.at[s, side, 3])
@@ -546,18 +568,42 @@
             along = (beyond - inside) if dx > 0 else (inside - beyond)
             value = 0.5 * (along + (py - my)) + isv * (level.k_up(z) - level.k_down(z))
             level.store(dv, 0 if dx < 0 else n + 1, 1, value * flag((dx, 0)))
+
+    def y_side_divergence(s, with_corners, level, u, mat, k, dv, dy_, xh, yh, ys, xm, ym):
+        cor = fcr if level is Fine else ccr
+        n = level.n
         for dy, side in side_of.items():
             x, z, beyond = yh[s, side, 0], yh[s, side, 2], yh[s, side, 3]
             inside = ys[s, side, 1]
             sub = plane_sub(level, x)
-            px = jnp.where(sub == n - 1, level.corner_plane(cor.at[s, corner_id[(1, dy)]], 0),
-                           plane_roll(level, x, -1))
-            mx = jnp.where(sub == 0, level.corner_plane(cor.at[s, corner_id[(-1, dy)]], 0),
-                           plane_roll(level, x, 1))
+            px, mx = plane_roll(level, x, -1), plane_roll(level, x, 1)
+            if with_corners:
+                px = jnp.where(sub == n - 1, level.corner_plane(cor.at[s, corner_id[(1, dy)]], 0), px)
+                mx = jnp.where(sub == 0, level.corner_plane(cor.at[s, corner_id[(-1, dy)]], 0), mx)
             isv = level.edge_scale(z.shape) / ym[side, 1]
             along = (beyond - inside) if dy > 0 else (inside - beyond)
             value = 0.5 * (along + (px - mx)) + isv * (level.plane_k_up(z) - level.plane_k_down(z))
             dy_[side] = value * flag((0, dy))
+
+    def middle(s, level, *rest):
+        n = level.n
+        y_side_divergence(s, False, level, *rest)
+        row_divergence(s, 1, 1, level, *rest)
+        for i in range(2, n - 2, R):
+            row_divergence(s, i, R, level, *rest)
+        row_divergence(s, n - 2, 1, level, *rest)
+        total = jnp.zeros((8, 128), F32)
+        for i in range(R, n - R, R):
+            total = total + rates(s, i, level, *rest)
+        return total
+
+    def outer(s, level, *rest):
+        n = level.n
+        x_side_divergence(s, level, *rest)
+        y_side_divergence(s, True, level, *rest)
+        for i in (0, n - 1):
+            row_divergence(s, i, 1, level, *rest)
+        return rates(s, 0, level, *rest) + rates(s, n - R, level, *rest)
 
     def fine_ghosts(s):
         sub, lane = subs((8, 128)), lanes((8, 128)) % 16
@@ -574,8 +620,8 @@
             return spread_row(ref[pl.ds(j, 1), :])
 
         def corner_rows(dx):
-            low, high = ccr.at[s, corner_id[(dx, -1)]], ccr.at[s, corner_id[(dx, 1)]]
-            return spread_row(low[4]), spread_row(high[4]), spread_row(high[5])
+            low, high = cpr.at[s, corner_id[(dx, -1)]], cpr.at[s, corner_id[(dx, 1)]]
+            return spread_row(low[0]), spread_row(high[0]), spread_row(high[1])
 
         own = shifted_rows(pls[s], row(ply.at[s, LO], 7), row(ply.at[s, HI], 0), row(ply.at[s, HI], 1))
         left = shifted_rows(plx[s, LO], *corner_rows(-1))
@@ -667,48 +713,47 @@
             energy = part if energy is None else energy + part
         return jnp.sum(coef[DM] * energy, axis=(0, 1))
 
-    def order(level):
-        n = level.n
-        return [0, n - R] + list(range(R, n - R, R))
-
     coarse_set, fine_set = levels
     for s in range(STEPS):
         last = s == STEPS - 1
-        receive(s, "cx", "cy", "co")
+        receive(s, "cy")
         if s == 0:
             receive(0, "mc")
             side_coefficients(Coarse, matc, kc, xmc, ymc)
             wait_load("coarse_prev")
-        divergences(s, *coarse_set)
-        total = jnp.zeros((8, 128), F32)
-        for m, i in enumerate(order(Coarse)):
-            total = total + rates(s, i, *coarse_set)
-            if m == 1 and not last:
-                pack_edge(s + 1)
-                send(s + 1, "cx", "co", "cp")
-        eacc[s, 1] = total
+        total = middle(s, *coarse_set)
+        receive(s, "co", "cx")
+        eacc[s, 1] = total + outer(s, *coarse_set)
         if not last:
+            pack_coarse_corners(s + 1)
+            send(s + 1, "co")
+            send(s + 1, "cx")
             pack_y(Coarse, s + 1)
             pack_plane(s + 1)
-            send(s + 1, "cy", "cq")
-        receive(s, "cp", "cq")
-        fine_ghosts(s)
-        receive(s, "fx", "fy", "fo")
+            send(s + 1, "cy", "cq", "cp")
+        receive(s, "cp", "cq", "fy")
         if s == 0:
             receive(0, "mf")
             side_coefficients(Fine, matf, kf, xmf, ymf)
             wait_load("fine_prev")
-        divergences(s, *fine_set)
-        total = jnp.zeros((8, 128), F32)
-        for m, i in enumerate(order(Fine)):
-            total = total + rates(s, i, *fine_set)
-            if m == 1 and not last:
-                pack_corners(s + 1)
-                send(s + 1, "fo", "fx")
-        eacc[s, 0] = total
+        fine_ghosts(s)
+        total = middle(s, *fine_set)
+        receive(s, "fo", "fx")
+        eacc[s, 0] = total + outer(s, *fine_set)
         if not last:
+            pack_corners(s + 1)
+            send(s + 1, "fo")
+            send(s + 1, "fx")
             pack_y(Fine, s + 1)
             send(s + 1, "fy")
+        if s == 0:
+            line_round(0)
+        if s == 1:
+            @pl.when(second)
+            def _():
+                line_wait(0)
+
+            line_round(1)
 
     lane1 = lanes((1, 128))
     row = jnp.zeros((1, 128), F32)
@@ -751,6 +796,7 @@
             plane = plane + er1[m]
         erow[1] = plane
         er2[gx_hi] = plane
+        line_wait(1)
         for d in far_first:
             for core in (0, 1):
                 pass_on(1, er2.at[gx_hi], {"gx": line_x[d], "gy": 2 * chip_y + core})
@@ -828,8 +874,10 @@
         vm((STEPS, 2, 8, 128), F32),
         vm((STEPS, 2, 8, 128), F32),
         vm((STEPS, 8, 128), F32),
-        vm((STEPS, 4, 6, 1, 128), F32),
-        vm((STEPS, 4, 6, 1, 128), F32),
+        vm((STEPS, 4, 4, 1, 128), F32),
+        vm((STEPS, 4, 4, 1, 128), F32),
+        vm((STEPS, 4, 2, 1, 128), F32),
+        vm((STEPS, 4, 2, 1, 128), F32),
         vm((STEPS, 4, 2, 1, 128), F32),
         vm((STEPS, 4, 2, 1, 128), F32),
         vm((2, 16, 16), jnp.int32),
@@ -840,10 +888,11 @@
         vm((max(n1, 2 * n2), 1, 128), F32),
         vm((max(n2, 1), 1, 128), F32),
         dma((13, 2)),
-        dma((STEPS, 32)),
-        dma((STEPS, 32)),
+        dma((STEPS, 36)),
+        dma((STEPS, 36)),
         dma((2,)),
         dma((2,)),
+        pltpu.SemaphoreType.REGULAR((2, 2)),
     ]
     anywhere = pl.BlockSpec(memory_space=pltpu.HBM)
     in_vmem = pl.BlockSpec(memory_space=pltpu.VMEM)

time: 38.3 us -> 38 us (level)
  Pallas kernels: 37.6 us -> 37.2 us
where the time goes in v3:
time: 38 us; the launch traced here: 37.9 us
  Pallas kernels  37.2 us (98%)
  between operations  0.64 us (2%)
    pallas_call x1, Pallas kernels, per_device(): pl.pallas_call(functools.partial(kernel, nx, ny, group_x), out_shape=out_...  36.4 us
    pallas_call x1, Pallas kernels, per_device(): pl.pallas_call(hand_out, out_shape=out_shape, in_specs=[in_vmem] * 3, out...  0.84 us

profile of v3, /device:TPU:1, one launch (start us, length us, event | category | flops | bytes accessed | tf_op | source)
XLA Modules:
  0.0 37.9 jit_solution(16158023558863158560)
XLA Ops:
  0.6 36.4 %leapfrog.1 = (f32[3,256,128]{2,1,0:T(8,128)S(1)}, f32[3,64,256]{2,1,0:T(8,128)S(1)}, f32[2,3]{1,0:T(2,128)S(1)}) custom-call(f32[3,256,128]{2,1,0:T(8,128)} %bitcast.15, f32[3,256,128]{2,1,0:T(8,128)} %bitcast.16, f32[3,64,256]{2,1,0:T(8,128)} %bitcast.17, f32[3,64,256]{2,1,0:T(8,128)} %bitcast.18, f32[256,128]{1,0:T(8,128)} %bitcast.19, ...), custom_call_target="tpu_custom_call" | custom-call | tf_op jit(solution)/shard_map/leapfrog/pallas_call | solution.py:904
  37.0 0.8 %hand_out.1 = (f32[3,256,128]{2,1,0:T(8,128)}, f32[3,64,256]{2,1,0:T(8,128)}, f32[2,3]{1,0:T(2,128)}) custom-call(f32[3,256,128]{2,1,0:T(8,128)S(1)} %get-tuple-element.9.refs_0_, f32[3,64,256]{2,1,0:T(8,128)S(1)} %get-tuple-element.10.refs_1_, f32[2,3]{1,0:T(2,128)S(1)} %get-tuple-element.11.refs_2_), custom_call_target="tpu_custom_call" | custom-call | tf_op jit(solution)/shard_map/hand_out/pallas_call | solution.py:915

commit v4 on v3

--- a/solution.py
+++ b/solution.py
@@ -351,20 +351,20 @@
             entries.append((group, d, copy))
         copies.append(entries)
 
-    def run(s, groups_wanted, what, backwards=False):
+    def run(s, groups_wanted, what, backwards=False, dx=None):
         for d in directions:
             mine = [c for g, e, c in copies[s] if g in groups_wanted and e == d]
-            if mine:
+            if mine and dx in (None, d[0]):
                 @pl.when(exists[(-d[0], -d[1]) if backwards else d])
                 def _(mine=mine):
                     for c in mine:
                         getattr(c(), what)()
 
-    def send(s, *wanted):
-        run(s, wanted, "start")
-
-    def receive(s, *wanted):
-        run(s, wanted, "wait_recv", backwards=True)
+    def send(s, *wanted, dx=None):
+        run(s, wanted, "start", dx=dx)
+
+    def receive(s, *wanted, side=None):
+        run(s, wanted, "wait_recv", backwards=True, dx=None if side is None else -side)
 
     def line_round(stage):
         steps = (by_one, by_two)[stage] if n2 > 3 else []
@@ -398,8 +398,10 @@
                 tile = jnp.where((lane == at) | (lane == at + 1), column, tile)
         return tile
 
-    def pack_coarse_corners(s):
+    def pack_coarse_corners(s, side):
         for (dx, dy), n in corner_id.items():
+            if dx != side:
+                continue
             ci, cj = (0 if dx < 0 else 7), (0 if dy < 0 else 7)
             for c in (0, 1):
                 for h in (0, 1):
@@ -413,8 +415,10 @@
             for m, j in enumerate((0, 1) if dy < 0 else (7, 7)):
                 cps[s, n, m] = edge[j : j + 1]
 
-    def pack_corners(s):
+    def pack_corners(s, side):
         for (dx, dy), n in corner_id.items():
+            if dx != side:
+                continue
             fi, fj = (0 if dx < 0 else 15), (0 if dy < 0 else 15)
             for c in (0, 1):
                 fcs[s, n, c] = uf[s + 1, c, pl.ds(16 * fi + fj, 1), :]
@@ -457,9 +461,10 @@
             ysmc[side, c] = Coarse.plane(matc.at[c], jc)
     pack_y(Fine, 0)
     pack_y(Coarse, 0)
-    pack_coarse_corners(0)
+    for dx in (-1, 1):
+        pack_coarse_corners(0, dx)
+        pack_corners(0, dx)
     pack_plane(0)
-    pack_corners(0)
 
     greeted = jnp.where(second, n1 // 2 + 2 * len(by_one), n1 // 2).astype(jnp.int32)
     for d in directions:
@@ -554,22 +559,22 @@
         value = 0.5 * ((px - mx) + (py - my)) + isv * (level.k_up(z) - level.k_down(z))
         level.store(dv, i + 1, r, value)
 
-    def x_side_divergence(s, level, u, mat, k, dv, dy_, xh, yh, ys, xm, ym):
+    def x_side_divergence(s, dx, level, u, mat, k, dv, dy_, xh, yh, ys, xm, ym):
         cor = fcr if level is Fine else ccr
         now, n = u.at[s + 1], level.n
-        for dx, side in side_of.items():
-            inside = level.load(now.at[0], 0 if dx < 0 else n - 1, 1)
-            beyond = halo_row(level, xh.at[s, side, 3])
-            y = halo_row(level, xh.at[s, side, 1])
-            z = halo_row(level, xh.at[s, side, 2])
-            py = level.j_up(y, level.corner_row(cor.at[s, corner_id[(dx, 1)]], 1))
-            my = level.j_down(y, level.corner_row(cor.at[s, corner_id[(dx, -1)]], 1))
-            isv = level.edge_scale(z.shape) / halo_row(level, xm.at[side, 1])
-            along = (beyond - inside) if dx > 0 else (inside - beyond)
-            value = 0.5 * (along + (py - my)) + isv * (level.k_up(z) - level.k_down(z))
-            level.store(dv, 0 if dx < 0 else n + 1, 1, value * flag((dx, 0)))
-
-    def y_side_divergence(s, with_corners, level, u, mat, k, dv, dy_, xh, yh, ys, xm, ym):
+        side = side_of[dx]
+        inside = level.load(now.at[0], 0 if dx < 0 else n - 1, 1)
+        beyond = halo_row(level, xh.at[s, side, 3])
+        y = halo_row(level, xh.at[s, side, 1])
+        z = halo_row(level, xh.at[s, side, 2])
+        py = level.j_up(y, level.corner_row(cor.at[s, corner_id[(dx, 1)]], 1))
+        my = level.j_down(y, level.corner_row(cor.at[s, corner_id[(dx, -1)]], 1))
+        isv = level.edge_scale(z.shape) / halo_row(level, xm.at[side, 1])
+        along = (beyond - inside) if dx > 0 else (inside - beyond)
+        value = 0.5 * (along + (py - my)) + isv * (level.k_up(z) - level.k_down(z))
+        level.store(dv, 0 if dx < 0 else n + 1, 1, value * flag((dx, 0)))
+
+    def y_side_divergence(s, known, level, u, mat, k, dv, dy_, xh, yh, ys, xm, ym):
         cor = fcr if level is Fine else ccr
         n = level.n
         for dy, side in side_of.items():
@@ -577,8 +582,9 @@
             inside = ys[s, side, 1]
             sub = plane_sub(level, x)
             px, mx = plane_roll(level, x, -1), plane_roll(level, x, 1)
-            if with_corners:
+            if 1 in known:
                 px = jnp.where(sub == n - 1, level.corner_plane(cor.at[s, corner_id[(1, dy)]], 0), px)
+            if -1 in known:
                 mx = jnp.where(sub == 0, level.corner_plane(cor.at[s, corner_id[(-1, dy)]], 0), mx)
             isv = level.edge_scale(z.shape) / ym[side, 1]
             along = (beyond - inside) if dy > 0 else (inside - beyond)
@@ -587,25 +593,32 @@
 
     def middle(s, level, *rest):
         n = level.n
-        y_side_divergence(s, False, level, *rest)
+        y_side_divergence(s, (), level, *rest)
         row_divergence(s, 1, 1, level, *rest)
         for i in range(2, n - 2, R):
             row_divergence(s, i, R, level, *rest)
         row_divergence(s, n - 2, 1, level, *rest)
         total = jnp.zeros((8, 128), F32)
-        for i in range(R, n - R, R):
+        for i in range(R, first_outer(level), R):
             total = total + rates(s, i, level, *rest)
         return total
 
-    def outer(s, level, *rest):
+    def first_outer(level):
+        return level.n - (4 if level is Fine else 2)
+
+    def outer(s, dx, level, *rest):
         n = level.n
-        x_side_divergence(s, level, *rest)
-        y_side_divergence(s, True, level, *rest)
-        for i in (0, n - 1):
-            row_divergence(s, i, 1, level, *rest)
-        return rates(s, 0, level, *rest) + rates(s, n - R, level, *rest)
-
-    def fine_ghosts(s):
+        x_side_divergence(s, dx, level, *rest)
+        y_side_divergence(s, (-1,) if dx < 0 else (-1, 1), level, *rest)
+        row_divergence(s, 0 if dx < 0 else n - 1, 1, level, *rest)
+        if dx < 0:
+            return rates(s, 0, level, *rest)
+        total = rates(s, n - R, level, *rest)
+        for i in range(first_outer(level), n - R, R):
+            total = total + rates(s, i, level, *rest)
+        return total
+
+    def fine_ghosts(s, known):
         sub, lane = subs((8, 128)), lanes((8, 128)) % 16
 
         def shifted_rows(tile, low, high0, high1):
@@ -624,20 +637,20 @@
             return spread_row(low[0]), spread_row(high[0]), spread_row(high[1])
 
         own = shifted_rows(pls[s], row(ply.at[s, LO], 7), row(ply.at[s, HI], 0), row(ply.at[s, HI], 1))
-        left = shifted_rows(plx[s, LO], *corner_rows(-1))
-        right = shifted_rows(plx[s, HI], *corner_rows(1))
+        if -1 in known:
+            left = shifted_rows(plx[s, LO], *corner_rows(-1))
+        if 1 in known:
+            right = shifted_rows(plx[s, HI], *corner_rows(1))
         totals = [jnp.zeros((8, 128), F32) for _ in (0, 1)]
         for mx in range(4):
             inner = [jnp.zeros((8, 128), F32) for _ in (0, 1)]
             for my in range(4):
-                if mx == 0:
-                    tile = jnp.where(lane < 2, roll(left[my], -14, 1), roll(own[my], 2, 1))
-                elif mx == 1:
-                    tile = own[my]
-                elif mx == 2:
-                    tile = jnp.where(lane >= 14, roll(right[my], 14, 1), roll(own[my], -2, 1))
-                else:
-                    tile = jnp.where(lane >= 12, roll(right[my], 12, 1), roll(own[my], -4, 1))
+                tile = roll(own[my], 2 - 2 * mx, 1) if mx != 1 else own[my]
+                if mx == 0 and -1 in known:
+                    tile = jnp.where(lane < 2, roll(left[my], -14, 1), tile)
+                if mx >= 2 and 1 in known:
+                    edge = 18 - 2 * mx
+                    tile = jnp.where(lane >= edge, roll(right[my], edge, 1), tile)
                 for t in (0, 1):
                     inner[t] = inner[t] + weights[t, 4 + my] * tile
             for t in (0, 1):
@@ -721,29 +734,36 @@
             receive(0, "mc")
             side_coefficients(Coarse, matc, kc, xmc, ymc)
             wait_load("coarse_prev")
-        total = middle(s, *coarse_set)
-        receive(s, "co", "cx")
-        eacc[s, 1] = total + outer(s, *coarse_set)
-        if not last:
-            pack_coarse_corners(s + 1)
-            send(s + 1, "co")
-            send(s + 1, "cx")
-            pack_y(Coarse, s + 1)
-            pack_plane(s + 1)
-            send(s + 1, "cy", "cq", "cp")
-        receive(s, "cp", "cq", "fy")
+        coarse_total = middle(s, *coarse_set)
+        receive(s, "cq", "fy")
         if s == 0:
             receive(0, "mf")
             side_coefficients(Fine, matf, kf, xmf, ymf)
             wait_load("fine_prev")
-        fine_ghosts(s)
-        total = middle(s, *fine_set)
-        receive(s, "fo", "fx")
-        eacc[s, 0] = total + outer(s, *fine_set)
+        fine_ghosts(s, ())
+        fine_total = middle(s, *fine_set)
+        for dx in (-1, 1):
+            receive(s, "co", "cx", side=dx)
+            coarse_total = coarse_total + outer(s, dx, *coarse_set)
+            if not last:
+                pack_coarse_corners(s + 1, dx)
+                send(s + 1, "co", dx=dx)
+                send(s + 1, "cx", dx=dx)
+        eacc[s, 1] = coarse_total
         if not last:
-            pack_corners(s + 1)
-            send(s + 1, "fo")
-            send(s + 1, "fx")
+            pack_y(Coarse, s + 1)
+            pack_plane(s + 1)
+            send(s + 1, "cy", "cq", "cp")
+        for dx in (-1, 1):
+            receive(s, "cp", "fo", "fx", side=dx)
+            fine_ghosts(s, (-1,) if dx < 0 else (-1, 1))
+            fine_total = fine_total + outer(s, dx, *fine_set)
+            if not last:
+                pack_corners(s + 1, dx)
+                send(s + 1, "fo", dx=dx)
+                send(s + 1, "fx", dx=dx)
+        eacc[s, 0] = fine_total
+        if not last:
             pack_y(Fine, s + 1)
             send(s + 1, "fy")
         if s == 0:

time: 38 us -> 38.5 us (1.013)
  Pallas kernels: 37.2 us -> 37.7 us
    pallas_call x1, Pallas kernels: 36.4 us -> 36.9 us  [per_device(): pl.pallas_call(functools.partial(kernel, nx, ny, group_x), out_shape=out_...]
where the time goes in v4:
time: 38.5 us; the launch traced here: 38.4 us
  Pallas kernels  37.7 us (98%)
  between operations  0.64 us (2%)
    pallas_call x1, Pallas kernels, per_device(): pl.pallas_call(functools.partial(kernel, nx, ny, group_x), out_shape=out_...  36.9 us
    pallas_call x1, Pallas kernels, per_device(): pl.pallas_call(hand_out, out_shape=out_shape, in_specs=[in_vmem] * 3, out...  0.84 us

profile of v4, /device:TPU:1, one launch (start us, length us, event | category | flops | bytes accessed | tf_op | source)
XLA Modules:
  0.0 38.4 jit_solution(17070692276424587787)
XLA Ops:
  0.6 36.9 %leapfrog.1 = (f32[3,256,128]{2,1,0:T(8,128)S(1)}, f32[3,64,256]{2,1,0:T(8,128)S(1)}, f32[2,3]{1,0:T(2,128)S(1)}) custom-call(f32[3,256,128]{2,1,0:T(8,128)} %bitcast.15, f32[3,256,128]{2,1,0:T(8,128)} %bitcast.16, f32[3,64,256]{2,1,0:T(8,128)} %bitcast.17, f32[3,64,256]{2,1,0:T(8,128)} %bitcast.18, f32[256,128]{1,0:T(8,128)} %bitcast.19, ...), custom_call_target="tpu_custom_call" | custom-call | tf_op jit(solution)/shard_map/leapfrog/pallas_call | solution.py:924
  37.5 0.8 %hand_out.1 = (f32[3,256,128]{2,1,0:T(8,128)}, f32[3,64,256]{2,1,0:T(8,128)}, f32[2,3]{1,0:T(2,128)}) custom-call(f32[3,256,128]{2,1,0:T(8,128)S(1)} %get-tuple-element.9.refs_0_, f32[3,64,256]{2,1,0:T(8,128)S(1)} %get-tuple-element.10.refs_1_, f32[2,3]{1,0:T(2,128)S(1)} %get-tuple-element.11.refs_2_), custom_call_target="tpu_custom_call" | custom-call | tf_op jit(solution)/shard_map/hand_out/pallas_call | solution.py:935

commit v5 on v4

--- a/solution.py
+++ b/solution.py
@@ -203,7 +203,7 @@
         uf, uc, matf, matc, kf, kc, dvf, dvc, dyf, dyc,
         xhf, xhc, yhf, yhc, ysf, ysc, xmf, xmc, ymf, ymc, ysmf, ysmc,
         pls, plx, ply, pex, ccs, ccr, cps, cpr, fcs, fcr, offsets_ref, weights, ghost, eacc, erow, er1, er2,
-        load_sem, send_sem, recv_sem, esend, erecv, line_sem,
+        load_sem, send_sem, recv_sem, esend, erecv, line_sem, plane_sem,
     ) = refs[16:]
 
     gx, gy = lax.axis_index("gx"), lax.axis_index("gy")
@@ -290,19 +290,6 @@
         def _(d=d):
             greet(device(d))
 
-    @pl.when(first_core)
-    def _():
-        greet({"gx": gx, "gy": 2 * chip_y + 1})
-
-    @pl.when(second)
-    def _():
-        for x in plane_x:
-            for y in plane_y:
-                if not (x is plane_x[0] and y is plane_y[0]):
-                    greet({"gx": x, "gy": y})
-                    greet({"gx": x, "gy": y + 1})
-        greet({"gx": gx, "gy": 2 * chip_y})
-
     side_of = {-1: LO, 1: HI}
 
     def messages(s):
@@ -319,17 +306,17 @@
             out.append(("cp", (dx, 0), pex.at[s], plx.at[s, far]))
             if s == 0:
                 first = 0 if dx < 0 else 15
-                out.append(("mf", (dx, 0), matf.at[pl.ds(0, 2), pl.ds(16 * first, 16)], xmf.at[far]))
+                out.append(("mfx", (dx, 0), matf.at[pl.ds(0, 2), pl.ds(16 * first, 16)], xmf.at[far]))
                 first = 0 if dx < 0 else 7
-                out.append(("mc", (dx, 0), matc.at[pl.ds(0, 2), :, pl.ds(8 * first, 8)], xmc.at[far]))
+                out.append(("mcx", (dx, 0), matc.at[pl.ds(0, 2), :, pl.ds(8 * first, 8)], xmc.at[far]))
         for dy in (-1, 1):
             own, far = side_of[dy], side_of[-dy]
             out.append(("fy", (0, dy), ysf.at[s, own], yhf.at[s, far]))
             out.append(("cy", (0, dy), ysc.at[s, own], yhc.at[s, far]))
             out.append(("cq", (0, dy), pls.at[s], ply.at[s, far]))
             if s == 0:
-                out.append(("mf", (0, dy), ysmf.at[own], ymf.at[far]))
-                out.append(("mc", (0, dy), ysmc.at[own], ymc.at[far]))
+                out.append(("mfy", (0, dy), ysmf.at[own], ymf.at[far]))
+                out.append(("mcy", (0, dy), ysmc.at[own], ymc.at[far]))
         for d in corners:
             back = corner_id[(-d[0], -d[1])]
             out.append(("co", d, ccs.at[s, corner_id[d]], ccr.at[s, back]))
@@ -366,20 +353,37 @@
     def receive(s, *wanted, side=None):
         run(s, wanted, "wait_recv", backwards=True, dx=None if side is None else -side)
 
-    def line_round(stage):
-        steps = (by_one, by_two)[stage] if n2 > 3 else []
-
-        @pl.when(second)
-        def _():
-            for m, d in enumerate(steps):
-                pl.semaphore_signal(
-                    line_sem.at[stage, m], inc=1,
-                    device_id={"gx": line_x[d], "gy": gy}, device_id_type=MESH,
-                )
-
-    def line_wait(stage):
-        for m in range(len((by_one, by_two)[stage]) if n2 > 3 else 0):
-            pl.semaphore_wait(line_sem.at[stage, m], 1)
+    def round_signals(stage):
+        away = 2 << stage
+        for side, ok, to in ((LO, gy + away < ny, gy + away), (HI, gy >= away, gy - away)):
+            if ny > 5:
+                @pl.when(ok)
+                def _(side=side, to=to):
+                    pl.semaphore_signal(
+                        plane_sem.at[stage, side], inc=1,
+                        device_id={"gx": gx, "gy": to}, device_id_type=MESH,
+                    )
+        if n2 > 3:
+            @pl.when(second)
+            def _():
+                for m, d in enumerate((by_one, by_two)[stage]):
+                    pl.semaphore_signal(
+                        line_sem.at[stage, m], inc=1,
+                        device_id={"gx": line_x[d], "gy": gy}, device_id_type=MESH,
+                    )
+
+    def round_wait(stage):
+        away = 2 << stage
+        for side, ok in ((LO, gy >= away), (HI, gy + away < ny)):
+            if ny > 5:
+                @pl.when(ok)
+                def _(side=side):
+                    pl.semaphore_wait(plane_sem.at[stage, side], 1)
+        if n2 > 3:
+            @pl.when(second)
+            def _():
+                for m in range(len((by_one, by_two)[stage])):
+                    pl.semaphore_wait(line_sem.at[stage, m], 1)
 
     def pack_y(level, s):
         u, out = (uf, ysf) if level is Fine else (uc, ysc)
@@ -466,15 +470,16 @@
         pack_corners(0, dx)
     pack_plane(0)
 
-    greeted = jnp.where(second, n1 // 2 + 2 * len(by_one), n1 // 2).astype(jnp.int32)
+    greeted = jnp.where(second, 2 * len(by_one), 0).astype(jnp.int32)
     for d in directions:
         greeted = greeted + jnp.where(exists[d], 1, 0).astype(jnp.int32)
     pl.semaphore_wait(barrier, greeted)
 
     send(0, "co")
-    send(0, "cx", "cy", "mc")
-    send(0, "fo", "fx", "fy", "mf")
-    send(0, "cp", "cq")
+    send(0, "cx", "mcx")
+    send(0, "cy", "mcy", "cq", "fy", "mfy")
+    send(0, "fo", "fx", "mfx")
+    send(0, "cp")
 
     wait_load("fine_density", "fine_lame", "coarse_density", "coarse_lame", "offsets")
     lane8 = lanes((8, 128))
@@ -525,23 +530,26 @@
             return Fine.load(ref, 0, 1)
         return Coarse.load(ref, 0, 1)
 
-    def side_coefficients(level, mat, k, xm, ym):
-        for i in range(0, level.n, R):
-            w = level.load(k.at[WIDE], i, R)
-            ha = level.load(k.at[HALF_A], i, R)
-
-            def outer(side):
-                return halo_row(level, xm.at[side, 0]) * halo_row(level, xm.at[side, 1])
-
-            cxp = ha * (w + neighbour_rows(level, k.at[WIDE], i, R, 1, lambda: outer(HI)))
-            cxm = ha * (w + neighbour_rows(level, k.at[WIDE], i, R, -1, lambda: outer(LO)))
-            up = level.row_of(ym.at[HI, 0], i, R) * level.row_of(ym.at[HI, 1], i, R)
-            down = level.row_of(ym.at[LO, 0], i, R) * level.row_of(ym.at[LO, 1], i, R)
-            cyu = ha * (w + level.j_up(w, up))
-            cyd = ha * (w + level.j_down(w, down))
-            total = cxp + cxm + cyu + cyd + level.load(k.at[CZU], i, R) + level.load(k.at[CZD], i, R)
-            for slot, value in ((CXP, cxp), (CXM, cxm), (CYU, cyu), (CYD, cyd), (C0, total)):
-                level.store(k.at[slot], i, R, value)
+    def side_coefficients(level, i, r, u, mat, k, dv, dy_, xh, yh, ys, xm, ym):
+        w = level.load(k.at[WIDE], i, r)
+        ha = level.load(k.at[HALF_A], i, r)
+
+        def outer(side):
+            return halo_row(level, xm.at[side, 0]) * halo_row(level, xm.at[side, 1])
+
+        cxp = ha * (w + neighbour_rows(level, k.at[WIDE], i, r, 1, lambda: outer(HI)))
+        cxm = ha * (w + neighbour_rows(level, k.at[WIDE], i, r, -1, lambda: outer(LO)))
+        up = level.row_of(ym.at[HI, 0], i, r) * level.row_of(ym.at[HI, 1], i, r)
+        down = level.row_of(ym.at[LO, 0], i, r) * level.row_of(ym.at[LO, 1], i, r)
+        cyu = ha * (w + level.j_up(w, up))
+        cyd = ha * (w + level.j_down(w, down))
+        total = cxp + cxm + cyu + cyd + level.load(k.at[CZU], i, r) + level.load(k.at[CZD], i, r)
+        for slot, value in ((CXP, cxp), (CXM, cxm), (CYU, cyu), (CYD, cyd), (C0, total)):
+            level.store(k.at[slot], i, r, value)
+
+    def inner_coefficients(level, *rest):
+        for i, r in [(1, 1)] + [(i, R) for i in range(2, level.n - 2, R)] + [(level.n - 2, 1)]:
+            side_coefficients(level, i, r, *rest)
 
     def row_divergence(s, i, r, level, u, mat, k, dv, dy_, xh, yh, ys, xm, ym):
         now = u.at[s + 1]
@@ -731,19 +739,22 @@
         last = s == STEPS - 1
         receive(s, "cy")
         if s == 0:
-            receive(0, "mc")
-            side_coefficients(Coarse, matc, kc, xmc, ymc)
+            receive(0, "mcy")
+            inner_coefficients(*coarse_set)
             wait_load("coarse_prev")
         coarse_total = middle(s, *coarse_set)
         receive(s, "cq", "fy")
         if s == 0:
-            receive(0, "mf")
-            side_coefficients(Fine, matf, kf, xmf, ymf)
+            receive(0, "mfy")
+            inner_coefficients(*fine_set)
             wait_load("fine_prev")
         fine_ghosts(s, ())
         fine_total = middle(s, *fine_set)
         for dx in (-1, 1):
             receive(s, "co", "cx", side=dx)
+            if s == 0:
+                receive(0, "mcx", side=dx)
+                side_coefficients(Coarse, 0 if dx < 0 else 7, 1, *coarse_set[1:])
             coarse_total = coarse_total + outer(s, dx, *coarse_set)
             if not last:
                 pack_coarse_corners(s + 1, dx)
@@ -756,6 +767,9 @@
             send(s + 1, "cy", "cq", "cp")
         for dx in (-1, 1):
             receive(s, "cp", "fo", "fx", side=dx)
+            if s == 0:
+                receive(0, "mfx", side=dx)
+                side_coefficients(Fine, 0 if dx < 0 else 15, 1, *fine_set[1:])
             fine_ghosts(s, (-1,) if dx < 0 else (-1, 1))
             fine_total = fine_total + outer(s, dx, *fine_set)
             if not last:
@@ -767,13 +781,12 @@
             pack_y(Fine, s + 1)
             send(s + 1, "fy")
         if s == 0:
-            line_round(0)
-        if s == 1:
-            @pl.when(second)
-            def _():
-                line_wait(0)
-
-            line_round(1)
+            round_signals(0)
+        elif s == 1:
+            round_wait(0)
+            round_signals(1)
+        else:
+            round_wait(1)
 
     lane1 = lanes((1, 128))
     row = jnp.zeros((1, 128), F32)
@@ -816,7 +829,6 @@
             plane = plane + er1[m]
         erow[1] = plane
         er2[gx_hi] = plane
-        line_wait(1)
         for d in far_first:
             for core in (0, 1):
                 pass_on(1, er2.at[gx_hi], {"gx": line_x[d], "gy": 2 * chip_y + core})
@@ -844,7 +856,7 @@
         rows(er1, n1 // 2, 0).wait_send()
 
     for s in range(STEPS):
-        run(s, ("co", "cp", "cq", "fo", "cx", "cy", "mc", "mf", "fx", "fy"), "wait_send")
+        run(s, ("co", "cp", "cq", "fo", "cx", "cy", "mcx", "mcy", "mfx", "mfy", "fx", "fy"), "wait_send")
 
 
 def hand_out(*refs):
@@ -913,6 +925,7 @@
         dma((2,)),
         dma((2,)),
         pltpu.SemaphoreType.REGULAR((2, 2)),
+        pltpu.SemaphoreType.REGULAR((2, 2)),
     ]
     anywhere = pl.BlockSpec(memory_space=pltpu.HBM)
     in_vmem = pl.BlockSpec(memory_space=pltpu.VMEM)

time: 38.5 us -> 37.3 us (0.969)
  Pallas kernels: 37.7 us -> 36.5 us
    pallas_call x1, Pallas kernels: 36.9 us -> 35.7 us  [per_device(): pl.pallas_call(functools.partial(kernel, nx, ny, group_x), out_shape=out_...]
where the time goes in v5:
time: 37.3 us; the launch traced here: 37.2 us
  Pallas kernels  36.5 us (98%)
  between operations  0.64 us (2%)
    pallas_call x1, Pallas kernels, per_device(): pl.pallas_call(functools.partial(kernel, nx, ny, group_x), out_shape=out_...  35.7 us
    pallas_call x1, Pallas kernels, per_device(): pl.pallas_call(hand_out, out_shape=out_shape, in_specs=[in_vmem] * 3, out...  0.84 us

profile of v5, /device:TPU:1, one launch (start us, length us, event | category | flops | bytes accessed | tf_op | source)
XLA Modules:
  0.0 37.2 jit_solution(3775633098202960030)
XLA Ops:
  0.6 35.7 %leapfrog.1 = (f32[3,256,128]{2,1,0:T(8,128)S(1)}, f32[3,64,256]{2,1,0:T(8,128)S(1)}, f32[2,3]{1,0:T(2,128)S(1)}) custom-call(f32[3,256,128]{2,1,0:T(8,128)} %bitcast.15, f32[3,256,128]{2,1,0:T(8,128)} %bitcast.16, f32[3,64,256]{2,1,0:T(8,128)} %bitcast.17, f32[3,64,256]{2,1,0:T(8,128)} %bitcast.18, f32[256,128]{1,0:T(8,128)} %bitcast.19, ...), custom_call_target="tpu_custom_call" | custom-call | tf_op jit(solution)/shard_map/leapfrog/pallas_call | solution.py:937
  36.3 0.8 %hand_out.1 = (f32[3,256,128]{2,1,0:T(8,128)}, f32[3,64,256]{2,1,0:T(8,128)}, f32[2,3]{1,0:T(2,128)}) custom-call(f32[3,256,128]{2,1,0:T(8,128)S(1)} %get-tuple-element.9.refs_0_, f32[3,64,256]{2,1,0:T(8,128)S(1)} %get-tuple-element.10.refs_1_, f32[2,3]{1,0:T(2,128)S(1)} %get-tuple-element.11.refs_2_), custom_call_target="tpu_custom_call" | custom-call | tf_op jit(solution)/shard_map/hand_out/pallas_call | solution.py:948

commit v6 on v5

--- a/solution.py
+++ b/solution.py
@@ -1,4 +1,5 @@
 import functools
+import math
 
 import jax
 import jax.numpy as jnp
@@ -202,7 +203,7 @@
     (
         uf, uc, matf, matc, kf, kc, dvf, dvc, dyf, dyc,
         xhf, xhc, yhf, yhc, ysf, ysc, xmf, xmc, ymf, ymc, ysmf, ysmc,
-        pls, plx, ply, pex, ccs, ccr, cps, cpr, fcs, fcr, offsets_ref, weights, ghost, eacc, erow, er1, er2,
+        pls, plx, ply, pex, ccs, ccr, fcs, fcr, sized, offsets_ref, weights, ghost, eacc, erow, er1, er2,
         load_sem, send_sem, recv_sem, esend, erecv, line_sem, plane_sem,
     ) = refs[16:]
 
@@ -235,45 +236,37 @@
     plane_y = [2 * lax.rem(chip_y + b, half) for b in range(half)]
     line_x = [lax.rem(gx_hi + d, n2) * group_x + gx_lo for d in range(n2)]
 
-    loads = {}
-
     def start_load(name, dst, sem):
-        fine = name.startswith("fine")
         src = hbm[name]
-        if fine:
-            copies = [pltpu.make_async_copy(src, dst, load_sem.at[sem, 0])]
-        else:
-            lead = (slice(None),) * (len(src.shape) - 2)
-            copies = [
-                pltpu.make_async_copy(
-                    src.at[lead + (slice(None), pl.ds(128 * h, 128))],
-                    dst.at[(slice(None), h) if lead else (h,)],
-                    load_sem.at[sem, h],
-                )
-                for h in (0, 1)
-            ]
-        for c in copies:
-            c.start()
-        loads[name] = copies
+        if name.startswith("fine"):
+            pltpu.make_async_copy(src, dst, load_sem.at[sem]).start()
+            return
+        lead = (slice(None),) * (len(src.shape) - 2)
+        for h in (0, 1):
+            pltpu.make_async_copy(
+                src.at[lead + (slice(None), pl.ds(128 * h, 128))],
+                dst.at[(slice(None), h) if lead else (h,)],
+                load_sem.at[sem],
+            ).start()
 
     plan = [
-        ("fine_disp", uf.at[1]), ("coarse_disp", uc.at[1]),
-        ("fine_rigidity", matf.at[0]), ("coarse_rigidity", matc.at[0]),
-        ("fine_metric", matf.at[1]), ("coarse_metric", matc.at[1]),
-        ("fine_density", matf.at[2]), ("fine_lame", matf.at[3]),
-        ("coarse_density", matc.at[2]), ("coarse_lame", matc.at[3]),
-        ("fine_prev", uf.at[0]), ("coarse_prev", uc.at[0]),
+        ("fine_disp", uf.at[1], 0), ("coarse_disp", uc.at[1], 1),
+        ("fine_rigidity", matf.at[0], 0), ("coarse_rigidity", matc.at[0], 1),
+        ("fine_metric", matf.at[1], 0), ("coarse_metric", matc.at[1], 1),
+        ("fine_density", matf.at[2], 2), ("fine_lame", matf.at[3], 2),
+        ("coarse_density", matc.at[2], 3), ("coarse_lame", matc.at[3], 3),
+        ("fine_prev", uf.at[0], 4), ("coarse_prev", uc.at[0], 5),
     ]
-    for sem, (name, dst) in enumerate(plan):
-        start_load(name, dst, sem)
-
-    loads["offsets"] = [pltpu.make_async_copy(offsets_hbm, offsets_ref, load_sem.at[12, 0])]
-    loads["offsets"][0].start()
-
-    def wait_load(*names):
-        for name in names:
-            for c in loads[name]:
-                c.wait()
+    for entry in plan:
+        start_load(*entry)
+    offsets_load = pltpu.make_async_copy(offsets_hbm, offsets_ref, load_sem.at[6])
+    offsets_load.start()
+    load_sizes = (kf.at[pl.ds(0, 5)], kc.at[pl.ds(0, 5)], kf.at[pl.ds(0, 2)], kc.at[pl.ds(0, 2)],
+                  kf.at[pl.ds(0, 3)], kc.at[pl.ds(0, 3)])
+
+    def wait_load(*sems):
+        for sem in sems:
+            pltpu.make_async_copy(load_sizes[sem], load_sizes[sem], load_sem.at[sem]).wait()
 
     barrier = pltpu.get_barrier_semaphore()
 
@@ -320,38 +313,57 @@
         for d in corners:
             back = corner_id[(-d[0], -d[1])]
             out.append(("co", d, ccs.at[s, corner_id[d]], ccr.at[s, back]))
-            out.append(("cp", d, cps.at[s, corner_id[d]], cpr.at[s, back]))
             out.append(("fo", d, fcs.at[s, corner_id[d]], fcr.at[s, back]))
         return out
 
-    copies = []
+    wait_with = {"cp": "fx", "mfx": "fx", "mcx": "cx", "cq": "fy", "mfy": "fy", "mcy": "cy"}
+    slots, copies, arriving, leaving = {}, [], [], dict.fromkeys(directions, 0)
     for s in range(STEPS):
-        entries = []
-        for n, (group, d, src, dst) in enumerate(messages(s)):
-            def copy(src=src, dst=dst, s=s, n=n, d=d):
+        entries, rows_of = [], {}
+        for group, d, src, dst in messages(s):
+            name = wait_with.get(group, group)
+            key = (s if name == "fx" else s % 2, name, d)
+            slot = slots.setdefault(key, len(slots))
+            rows = math.prod(src.shape) // 128
+            rows_of[key] = rows_of.get(key, 0) + rows
+            leaving[d] += rows
+
+            def copy(src=src, dst=dst, slot=slot, d=d):
                 return pltpu.make_async_remote_copy(
                     src_ref=src, dst_ref=dst,
-                    send_sem=send_sem.at[s, n], recv_sem=recv_sem.at[s, n],
+                    send_sem=send_sem.at[directions.index(d)], recv_sem=recv_sem.at[slot],
                     device_id=device(d), device_id_type=MESH,
                 )
 
             entries.append((group, d, copy))
         copies.append(entries)
-
-    def run(s, groups_wanted, what, backwards=False, dx=None):
+        arriving.append(rows_of)
+
+    def bytes_of(rows, d, slot):
+        part = sized.at[pl.ds(0, rows)]
+        return pltpu.make_async_remote_copy(
+            src_ref=part, dst_ref=part,
+            send_sem=send_sem.at[directions.index(d)], recv_sem=recv_sem.at[slot],
+            device_id=device(d), device_id_type=MESH,
+        )
+
+    def send(s, *wanted, dx=None):
         for d in directions:
-            mine = [c for g, e, c in copies[s] if g in groups_wanted and e == d]
+            mine = [c for g, e, c in copies[s] if g in wanted and e == d]
             if mine and dx in (None, d[0]):
-                @pl.when(exists[(-d[0], -d[1]) if backwards else d])
+                @pl.when(exists[d])
                 def _(mine=mine):
                     for c in mine:
-                        getattr(c(), what)()
-
-    def send(s, *wanted, dx=None):
-        run(s, wanted, "start", dx=dx)
+                        c().start()
 
     def receive(s, *wanted, side=None):
-        run(s, wanted, "wait_recv", backwards=True, dx=None if side is None else -side)
+        for d in directions:
+            mine = [k for k in arriving[s] if k[1] in wanted and k[2] == d]
+            if mine and (side is None or d[0] == -side):
+                @pl.when(exists[(-d[0], -d[1])])
+                def _(mine=mine, d=d):
+                    for k in mine:
+                        bytes_of(arriving[s][k], d, slots[k]).wait_recv()
 
     def round_signals(stage):
         away = 2 << stage
@@ -417,7 +429,7 @@
         pls[s] = plane_tile(s, edge, range(2, 7))
         for (dx, dy), n in corner_id.items():
             for m, j in enumerate((0, 1) if dy < 0 else (7, 7)):
-                cps[s, n, m] = edge[j : j + 1]
+                fcs[s, n, 2 + m] = edge[j : j + 1]
 
     def pack_corners(s, side):
         for (dx, dy), n in corner_id.items():
@@ -454,11 +466,9 @@
         def _(n=corner_id[d]):
             for s in range(STEPS):
                 ccr[s, n] = jnp.zeros(ccr.shape[2:], F32)
-                cpr[s, n] = jnp.zeros(cpr.shape[2:], F32)
                 fcr[s, n] = jnp.zeros(fcr.shape[2:], F32)
 
-    wait_load("fine_disp", "coarse_disp", "fine_rigidity", "coarse_rigidity", "fine_metric",
-              "coarse_metric")
+    wait_load(0, 1)
     for c in (0, 1):
         for side, jf, jc in ((LO, 0, 0), (HI, 15, 7)):
             ysmf[side, c] = Fine.plane(matf.at[c], jf)
@@ -481,7 +491,8 @@
     send(0, "fo", "fx", "mfx")
     send(0, "cp")
 
-    wait_load("fine_density", "fine_lame", "coarse_density", "coarse_lame", "offsets")
+    wait_load(2, 3)
+    offsets_load.wait()
     lane8 = lanes((8, 128))
     spread = jnp.where(
         (lanes((16, 128)) % 16 == subs((16, 128))) & (lanes((16, 128)) < 48), 1.0, 0.0
@@ -641,8 +652,8 @@
             return spread_row(ref[pl.ds(j, 1), :])
 
         def corner_rows(dx):
-            low, high = cpr.at[s, corner_id[(dx, -1)]], cpr.at[s, corner_id[(dx, 1)]]
-            return spread_row(low[0]), spread_row(high[0]), spread_row(high[1])
+            low, high = fcr.at[s, corner_id[(dx, -1)]], fcr.at[s, corner_id[(dx, 1)]]
+            return spread_row(low[2]), spread_row(high[2]), spread_row(high[3])
 
         own = shifted_rows(pls[s], row(ply.at[s, LO], 7), row(ply.at[s, HI], 0), row(ply.at[s, HI], 1))
         if -1 in known:
@@ -739,21 +750,18 @@
         last = s == STEPS - 1
         receive(s, "cy")
         if s == 0:
-            receive(0, "mcy")
             inner_coefficients(*coarse_set)
-            wait_load("coarse_prev")
+            wait_load(5)
         coarse_total = middle(s, *coarse_set)
-        receive(s, "cq", "fy")
+        receive(s, "fy")
         if s == 0:
-            receive(0, "mfy")
             inner_coefficients(*fine_set)
-            wait_load("fine_prev")
+            wait_load(4)
         fine_ghosts(s, ())
         fine_total = middle(s, *fine_set)
         for dx in (-1, 1):
             receive(s, "co", "cx", side=dx)
             if s == 0:
-                receive(0, "mcx", side=dx)
                 side_coefficients(Coarse, 0 if dx < 0 else 7, 1, *coarse_set[1:])
             coarse_total = coarse_total + outer(s, dx, *coarse_set)
             if not last:
@@ -766,9 +774,8 @@
             pack_plane(s + 1)
             send(s + 1, "cy", "cq", "cp")
         for dx in (-1, 1):
-            receive(s, "cp", "fo", "fx", side=dx)
+            receive(s, "fo", "fx", side=dx)
             if s == 0:
-                receive(0, "mfx", side=dx)
                 side_coefficients(Fine, 0 if dx < 0 else 15, 1, *fine_set[1:])
             fine_ghosts(s, (-1,) if dx < 0 else (-1, 1))
             fine_total = fine_total + outer(s, dx, *fine_set)
@@ -855,8 +862,10 @@
     def _():
         rows(er1, n1 // 2, 0).wait_send()
 
-    for s in range(STEPS):
-        run(s, ("co", "cp", "cq", "fo", "cx", "cy", "mcx", "mcy", "mfx", "mfy", "fx", "fy"), "wait_send")
+    for d in directions:
+        @pl.when(exists[d])
+        def _(d=d):
+            bytes_of(leaving[d], d, 0).wait_send()
 
 
 def hand_out(*refs):
@@ -908,10 +917,9 @@
         vm((STEPS, 8, 128), F32),
         vm((STEPS, 4, 4, 1, 128), F32),
         vm((STEPS, 4, 4, 1, 128), F32),
-        vm((STEPS, 4, 2, 1, 128), F32),
-        vm((STEPS, 4, 2, 1, 128), F32),
-        vm((STEPS, 4, 2, 1, 128), F32),
-        vm((STEPS, 4, 2, 1, 128), F32),
+        vm((STEPS, 4, 4, 1, 128), F32),
+        vm((STEPS, 4, 4, 1, 128), F32),
+        vm((480, 128), F32),
         vm((2, 16, 16), jnp.int32),
         vm((2, 8, 8, 128), F32),
         vm((2, 8, 128), F32),
@@ -919,9 +927,9 @@
         vm((2, 1, 128), F32),
         vm((max(n1, 2 * n2), 1, 128), F32),
         vm((max(n2, 1), 1, 128), F32),
-        dma((13, 2)),
-        dma((STEPS, 36)),
-        dma((STEPS, 36)),
+        dma((7,)),
+        dma((8,)),
+        dma((34,)),
         dma((2,)),
         dma((2,)),
         pltpu.SemaphoreType.REGULAR((2, 2)),

time: 37.3 us -> 35.4 us (0.949)
  Pallas kernels: 36.5 us -> 34.7 us
    pallas_call x1, Pallas kernels: 35.7 us -> 33.9 us  [per_device(): pl.pallas_call(functools.partial(kernel, nx, ny, group_x), out_shape=out_...]
where the time goes in v6:
time: 35.4 us; the launch traced here: 35.3 us
  Pallas kernels  34.7 us (98%)
  between operations  0.64 us (2%)
    pallas_call x1, Pallas kernels, per_device(): pl.pallas_call(functools.partial(kernel, nx, ny, group_x), out_shape=out_...  33.9 us
    pallas_call x1, Pallas kernels, per_device(): pl.pallas_call(hand_out, out_shape=out_shape, in_specs=[in_vmem] * 3, out...  0.84 us

profile of v6, /device:TPU:1, one launch (start us, length us, event | category | flops | bytes accessed | tf_op | source)
XLA Modules:
  0.0 35.3 jit_solution(3262820538413559535)
XLA Ops:
  0.6 33.9 %leapfrog.1 = (f32[3,256,128]{2,1,0:T(8,128)S(1)}, f32[3,64,256]{2,1,0:T(8,128)S(1)}, f32[2,3]{1,0:T(2,128)S(1)}) custom-call(f32[3,256,128]{2,1,0:T(8,128)} %bitcast.15, f32[3,256,128]{2,1,0:T(8,128)} %bitcast.16, f32[3,64,256]{2,1,0:T(8,128)} %bitcast.17, f32[3,64,256]{2,1,0:T(8,128)} %bitcast.18, f32[256,128]{1,0:T(8,128)} %bitcast.19, ...), custom_call_target="tpu_custom_call" | custom-call | tf_op jit(solution)/shard_map/leapfrog/pallas_call | solution.py:945
  34.5 0.8 %hand_out.1 = (f32[3,256,128]{2,1,0:T(8,128)}, f32[3,64,256]{2,1,0:T(8,128)}, f32[2,3]{1,0:T(2,128)}) custom-call(f32[3,256,128]{2,1,0:T(8,128)S(1)} %get-tuple-element.9.refs_0_, f32[3,64,256]{2,1,0:T(8,128)S(1)} %get-tuple-element.10.refs_1_, f32[2,3]{1,0:T(2,128)S(1)} %get-tuple-element.11.refs_2_), custom_call_target="tpu_custom_call" | custom-call | tf_op jit(solution)/shard_map/hand_out/pallas_call | solution.py:956

commit v7 on v6

--- a/solution.py
+++ b/solution.py
@@ -316,13 +316,13 @@
             out.append(("fo", d, fcs.at[s, corner_id[d]], fcr.at[s, back]))
         return out
 
-    wait_with = {"cp": "fx", "mfx": "fx", "mcx": "cx", "cq": "fy", "mfy": "fy", "mcy": "cy"}
+    wait_with = {"mfx": "fx", "mcx": "cx", "cq": "fy", "mfy": "fy", "mcy": "cy"}
     slots, copies, arriving, leaving = {}, [], [], dict.fromkeys(directions, 0)
     for s in range(STEPS):
         entries, rows_of = [], {}
         for group, d, src, dst in messages(s):
             name = wait_with.get(group, group)
-            key = (s if name == "fx" else s % 2, name, d)
+            key = (s if name == "cp" else s % 2, name, d)
             slot = slots.setdefault(key, len(slots))
             rows = math.prod(src.shape) // 128
             rows_of[key] = rows_of.get(key, 0) + rows
@@ -485,11 +485,17 @@
         greeted = greeted + jnp.where(exists[d], 1, 0).astype(jnp.int32)
     pl.semaphore_wait(barrier, greeted)
 
-    send(0, "co")
-    send(0, "cx", "mcx")
+    def send_first_x():
+        send(0, "cx", "mcx")
+        send(0, "cp", "fx", "mfx")
+
+    send(0, "co", "fo")
+
+    @pl.when(first_core)
+    def _():
+        send_first_x()
+
     send(0, "cy", "mcy", "cq", "fy", "mfy")
-    send(0, "fo", "fx", "mfx")
-    send(0, "cp")
 
     wait_load(2, 3)
     offsets_load.wait()
@@ -536,6 +542,10 @@
             ):
                 level.store(k.at[slot], i, R, value)
 
+    @pl.when(second)
+    def _():
+        send_first_x()
+
     def halo_row(level, ref):
         if level is Fine:
             return Fine.load(ref, 0, 1)
@@ -630,12 +640,7 @@
         x_side_divergence(s, dx, level, *rest)
         y_side_divergence(s, (-1,) if dx < 0 else (-1, 1), level, *rest)
         row_divergence(s, 0 if dx < 0 else n - 1, 1, level, *rest)
-        if dx < 0:
-            return rates(s, 0, level, *rest)
-        total = rates(s, n - R, level, *rest)
-        for i in range(first_outer(level), n - R, R):
-            total = total + rates(s, i, level, *rest)
-        return total
+        return rates(s, 0 if dx < 0 else n - R, level, *rest)
 
     def fine_ghosts(s, known):
         sub, lane = subs((8, 128)), lanes((8, 128)) % 16
@@ -773,11 +778,13 @@
             pack_y(Coarse, s + 1)
             pack_plane(s + 1)
             send(s + 1, "cy", "cq", "cp")
+        receive(s, "cp", "fo")
+        fine_ghosts(s, (-1, 1))
+        fine_total = fine_total + rates(s, first_outer(Fine), *fine_set)
         for dx in (-1, 1):
-            receive(s, "fo", "fx", side=dx)
+            receive(s, "fx", side=dx)
             if s == 0:
                 side_coefficients(Fine, 0 if dx < 0 else 15, 1, *fine_set[1:])
-            fine_ghosts(s, (-1,) if dx < 0 else (-1, 1))
             fine_total = fine_total + outer(s, dx, *fine_set)
             if not last:
                 pack_corners(s + 1, dx)
@@ -929,7 +936,7 @@
         vm((max(n2, 1), 1, 128), F32),
         dma((7,)),
         dma((8,)),
-        dma((34,)),
+        dma((38,)),
         dma((2,)),
         dma((2,)),
         pltpu.SemaphoreType.REGULAR((2, 2)),

time: 35.4 us -> 35.2 us (level)
  no operation moved by 1% of the time
where the time goes in v7:
time: 35.2 us; the launch traced here: 35.1 us
  Pallas kernels  34.5 us (98%)
  between operations  0.64 us (2%)
    pallas_call x1, Pallas kernels, per_device(): pl.pallas_call(functools.partial(kernel, nx, ny, group_x), out_shape=out_...  33.7 us
    pallas_call x1, Pallas kernels, per_device(): pl.pallas_call(hand_out, out_shape=out_shape, in_specs=[in_vmem] * 3, out...  0.84 us

profile of v7, /device:TPU:1, one launch (start us, length us, event | category | flops | bytes accessed | tf_op | source)
XLA Modules:
  0.0 35.1 jit_solution(1876192947430946567)
XLA Ops:
  0.6 33.7 %leapfrog.1 = (f32[3,256,128]{2,1,0:T(8,128)S(1)}, f32[3,64,256]{2,1,0:T(8,128)S(1)}, f32[2,3]{1,0:T(2,128)S(1)}) custom-call(f32[3,256,128]{2,1,0:T(8,128)} %bitcast.15, f32[3,256,128]{2,1,0:T(8,128)} %bitcast.16, f32[3,64,256]{2,1,0:T(8,128)} %bitcast.17, f32[3,64,256]{2,1,0:T(8,128)} %bitcast.18, f32[256,128]{1,0:T(8,128)} %bitcast.19, ...), custom_call_target="tpu_custom_call" | custom-call | tf_op jit(solution)/shard_map/leapfrog/pallas_call | solution.py:952
  34.3 0.8 %hand_out.1 = (f32[3,256,128]{2,1,0:T(8,128)}, f32[3,64,256]{2,1,0:T(8,128)}, f32[2,3]{1,0:T(2,128)}) custom-call(f32[3,256,128]{2,1,0:T(8,128)S(1)} %get-tuple-element.9.refs_0_, f32[3,64,256]{2,1,0:T(8,128)S(1)} %get-tuple-element.10.refs_1_, f32[2,3]{1,0:T(2,128)S(1)} %get-tuple-element.11.refs_2_), custom_call_target="tpu_custom_call" | custom-call | tf_op jit(solution)/shard_map/hand_out/pallas_call | solution.py:963

commit v8 on v7

--- a/solution.py
+++ b/solution.py
@@ -638,7 +638,6 @@
     def outer(s, dx, level, *rest):
         n = level.n
         x_side_divergence(s, dx, level, *rest)
-        y_side_divergence(s, (-1,) if dx < 0 else (-1, 1), level, *rest)
         row_divergence(s, 0 if dx < 0 else n - 1, 1, level, *rest)
         return rates(s, 0 if dx < 0 else n - R, level, *rest)
 
@@ -764,8 +763,10 @@
             wait_load(4)
         fine_ghosts(s, ())
         fine_total = middle(s, *fine_set)
+        receive(s, "co")
+        y_side_divergence(s, (-1, 1), *coarse_set)
         for dx in (-1, 1):
-            receive(s, "co", "cx", side=dx)
+            receive(s, "cx", side=dx)
             if s == 0:
                 side_coefficients(Coarse, 0 if dx < 0 else 7, 1, *coarse_set[1:])
             coarse_total = coarse_total + outer(s, dx, *coarse_set)
@@ -780,8 +781,9 @@
             send(s + 1, "cy", "cq", "cp")
         receive(s, "cp", "fo")
         fine_ghosts(s, (-1, 1))
+        y_side_divergence(s, (-1, 1), *fine_set)
         fine_total = fine_total + rates(s, first_outer(Fine), *fine_set)
-        for dx in (-1, 1):
+        for dx in (1, -1) if last else (-1, 1):
             receive(s, "fx", side=dx)
             if s == 0:
                 side_coefficients(Fine, 0 if dx < 0 else 15, 1, *fine_set[1:])

time: 35.2 us -> 35.1 us (level)
  no operation moved by 1% of the time
where the time goes in v8:
time: 35.1 us; the launch traced here: 35 us
  Pallas kernels  34.3 us (98%)
  between operations  0.64 us (2%)
    pallas_call x1, Pallas kernels, per_device(): pl.pallas_call(functools.partial(kernel, nx, ny, group_x), out_shape=out_...  33.5 us
    pallas_call x1, Pallas kernels, per_device(): pl.pallas_call(hand_out, out_shape=out_shape, in_specs=[in_vmem] * 3, out...  0.84 us

profile of v8, /device:TPU:1, one launch (start us, length us, event | category | flops | bytes accessed | tf_op | source)
XLA Modules:
  0.0 35.0 jit_solution(7949566464694705357)
XLA Ops:
  0.6 33.5 %leapfrog.1 = (f32[3,256,128]{2,1,0:T(8,128)S(1)}, f32[3,64,256]{2,1,0:T(8,128)S(1)}, f32[2,3]{1,0:T(2,128)S(1)}) custom-call(f32[3,256,128]{2,1,0:T(8,128)} %bitcast.15, f32[3,256,128]{2,1,0:T(8,128)} %bitcast.16, f32[3,64,256]{2,1,0:T(8,128)} %bitcast.17, f32[3,64,256]{2,1,0:T(8,128)} %bitcast.18, f32[256,128]{1,0:T(8,128)} %bitcast.19, ...), custom_call_target="tpu_custom_call" | custom-call | tf_op jit(solution)/shard_map/leapfrog/pallas_call | solution.py:954
  34.1 0.8 %hand_out.1 = (f32[3,256,128]{2,1,0:T(8,128)}, f32[3,64,256]{2,1,0:T(8,128)}, f32[2,3]{1,0:T(2,128)}) custom-call(f32[3,256,128]{2,1,0:T(8,128)S(1)} %get-tuple-element.9.refs_0_, f32[3,64,256]{2,1,0:T(8,128)S(1)} %get-tuple-element.10.refs_1_, f32[2,3]{1,0:T(2,128)S(1)} %get-tuple-element.11.refs_2_), custom_call_target="tpu_custom_call" | custom-call | tf_op jit(solution)/shard_map/hand_out/pallas_call | solution.py:965

commit v9 on v8

--- a/solution.py
+++ b/solution.py
@@ -878,7 +878,9 @@
 
 
 def hand_out(*refs):
-    copies = [pltpu.make_async_copy(refs[n], refs[3 + n], refs[6].at[n]) for n in range(3)]
+    pairs = [(refs[n].at[c], refs[3 + n].at[c]) for n in (0, 1) for c in range(3)]
+    pairs.append((refs[2], refs[5]))
+    copies = [pltpu.make_async_copy(a, b, refs[6].at[n]) for n, (a, b) in enumerate(pairs)]
     for c in copies:
         c.start()
     for c in copies:
@@ -967,7 +969,7 @@
         out_shape=out_shape,
         in_specs=[in_vmem] * 3,
         out_specs=[anywhere] * 3,
-        scratch_shapes=[dma((3,))],
+        scratch_shapes=[dma((7,))],
         compiler_params=pltpu.CompilerParams(vmem_limit_bytes=1 << 20),
         name="hand_out",
     )(*results)

time: 35.1 us -> 35.1 us (level)
  no operation moved by 1% of the time
where the time goes in v9:
time: 35.1 us; the launch traced here: 35 us
  Pallas kernels  34.4 us (98%)
  between operations  0.64 us (2%)
    pallas_call x1, Pallas kernels, per_device(): pl.pallas_call(functools.partial(kernel, nx, ny, group_x), out_shape=out_...  33.5 us
    pallas_call x1, Pallas kernels, per_device(): pl.pallas_call(hand_out, out_shape=out_shape, in_specs=[in_vmem] * 3, out...  0.87 us

profile of v9, /device:TPU:1, one launch (start us, length us, event | category | flops | bytes accessed | tf_op | source)
XLA Modules:
  0.0 35.0 jit_solution(4814132482902215215)
XLA Ops:
  0.6 33.5 %leapfrog.1 = (f32[3,256,128]{2,1,0:T(8,128)S(1)}, f32[3,64,256]{2,1,0:T(8,128)S(1)}, f32[2,3]{1,0:T(2,128)S(1)}) custom-call(f32[3,256,128]{2,1,0:T(8,128)} %bitcast.15, f32[3,256,128]{2,1,0:T(8,128)} %bitcast.16, f32[3,64,256]{2,1,0:T(8,128)} %bitcast.17, f32[3,64,256]{2,1,0:T(8,128)} %bitcast.18, f32[256,128]{1,0:T(8,128)} %bitcast.19, ...), custom_call_target="tpu_custom_call" | custom-call | tf_op jit(solution)/shard_map/leapfrog/pallas_call | solution.py:956
  34.1 0.9 %hand_out.1 = (f32[3,256,128]{2,1,0:T(8,128)}, f32[3,64,256]{2,1,0:T(8,128)}, f32[2,3]{1,0:T(2,128)}) custom-call(f32[3,256,128]{2,1,0:T(8,128)S(1)} %get-tuple-element.9.refs_0_, f32[3,64,256]{2,1,0:T(8,128)S(1)} %get-tuple-element.10.refs_1_, f32[2,3]{1,0:T(2,128)S(1)} %get-tuple-element.11.refs_2_), custom_call_target="tpu_custom_call" | custom-call | tf_op jit(solution)/shard_map/hand_out/pallas_call | solution.py:967
